TPU v7x, 128 devices: a whole 4x4x4 slice. The times are simulated.
128 devices in a mesh: blk: 64 (over y_lo, z, x, core), rep: 2 (over y_hi).
Axes of the slice: x: 4, y: 4 (y_hi: 2, y_lo: 2; y = y_hi * 2 + y_lo), z: 4, core: 2. Of those that a mesh axis runs over, the one named last changes fastest.
Arguments:
- measured: float32 [3, 64, 8, 1536], P(None, 'blk', None, 'rep'), may hold values from -4 to 4
- rot_vector: float32 [3, 64, 8, 1536], P(None, 'blk', None, 'rep'), may hold values from -6 to 6
- confidence: float32 [3, 64, 8, 1536], P(None, 'blk', None, 'rep'), may hold values from 0.5 to 2
- first_local: int32 [64, 8, 1536], P('blk', None, 'rep'), may hold values from 0 to 2047
- second_local: int32 [64, 8, 1536], P('blk', None, 'rep'), may hold values from 0 to 2047
- edge_counts: int32 [64, 8, 2], P('blk', None, 'rep'), may hold values from 256 to 768, as said below
- start_angles: float32 [3, 131072], P(None, 'blk'), may hold values from -4 to 4
- anchor: float32 [131072], P('blk'), may hold values from 0.05 to 0.5
Outputs:
- estimate: float32 [3, 131072], P(None, 'blk')
- weights: float32 [64, 8, 1536], P('blk', None, 'rep')
Inputs may be any that keep to these rules, and one draw needn't show every extreme that they name: `edge_counts`: live edges of a tile pair on one device fill its first slots; in every tile some pair holds 768 live edges on one device.
All inputs are finite; a program needn't handle non-finite values.
Results may differ from a plain program's by a relative error of at most 0.0001.
Values sent between devices are 32-bit elements; how exact they have to be, the bound alone decides.
A program may use at most 128 MiB of HBM per device.

v0:
```python
import jax
import jax.numpy as jnp
from jax import lax
from jax.sharding import PartitionSpec as P

PASSES = 2
ITERS = 2


PAIRS = ((0, 0), (0, 1), (0, 2), (1, 1), (1, 2), (2, 2))
LOOKUP = ((0, 1, 2), (1, 3, 4), (2, 4, 5))
SOFTEN = 0.05


def shifted(value, axis, steps):
    count = lax.axis_size(axis)
    pairs = [(source, (source + steps) % count) for source in range(count)]
    return lax.ppermute(value, axis, pairs)


def gathered_total(array, axis):
    return lax.all_gather(array, axis).sum(0)


def from_everyone(array, axis):
    peers = lax.axis_size(axis)
    return lax.all_to_all(
        jnp.broadcast_to(array[None], (peers, *array.shape)), axis, 0, 0, tiled=True
    )


def taken_together(array, axis):
    everything = from_everyone(array, axis)
    return jnp.sum(everything, axis=0)


def rotations(vector):
    squared = vector[0] * vector[0] + vector[1] * vector[1] + vector[2] * vector[2]
    factor = 2.0 / (1.0 + squared)
    zeros = jnp.zeros_like(squared)
    skewed = (
        (zeros, -vector[2], vector[1]),
        (vector[2], zeros, -vector[0]),
        (-vector[1], vector[0], zeros),
    )
    matrix_rows = []
    for first in range(3):
        entries = []
        for second in range(3):
            term = skewed[first][second] + vector[first] * vector[second]
            if first == second:
                entries.append(1.0 + factor * (term - squared))
            else:
                entries.append(factor * term)
        matrix_rows.append(jnp.stack(entries))
    return jnp.stack(matrix_rows)


def rotate(rotation, vector):
    return jnp.sum(rotation * vector[None], axis=1)


def rotate_back(rotation, vector):
    return jnp.sum(rotation * vector[:, None], axis=0)


def block_parts(weighted, rotation):
    far_list = []
    near_list = []
    for first, second in PAIRS:
        near_list.append(jnp.sum(rotation[:, first] * weighted * rotation[:, second], axis=0))
        if first == second:
            far_list.append(weighted[first])
        else:
            far_list.append(jnp.zeros_like(weighted[0]))
    return (jnp.stack(far_list), jnp.stack(near_list))


def inverse_apply(blocks, vector):
    adjugate = jnp.stack(
        [
            blocks[3] * blocks[5] - blocks[4] * blocks[4],
            blocks[2] * blocks[4] - blocks[1] * blocks[5],
            blocks[1] * blocks[4] - blocks[2] * blocks[3],
            blocks[0] * blocks[5] - blocks[2] * blocks[2],
            blocks[1] * blocks[2] - blocks[0] * blocks[4],
            blocks[0] * blocks[3] - blocks[1] * blocks[1],
        ]
    )
    determinant = blocks[0] * adjugate[0] + blocks[1] * adjugate[1] + blocks[2] * adjugate[2]
    result = []
    for first in range(3):
        total = (
            adjugate[LOOKUP[first][0]] * vector[0]
            + adjugate[LOOKUP[first][1]] * vector[1]
            + adjugate[LOOKUP[first][2]] * vector[2]
        )
        result.append(total / determinant)
    return jnp.stack(result)


def spread(terms, index, total):
    return jax.vmap(lambda values: jax.ops.segment_sum(values, index, num_segments=total))(terms)


def on_device(
    measured, rot_vector, confidence, first_local, second_local, edge_counts, start_angles, anchor
):
    tile_cams = start_angles.shape[1]
    pair_count = first_local.shape[1]
    slot_count = first_local.shape[2]
    window_span = pair_count * tile_cams
    first = first_local.reshape(-1)
    second = (
        jnp.arange(pair_count, dtype=jnp.int32)[:, None] * tile_cams + second_local[0]
    ).reshape(-1)
    live = (
        (jnp.arange(slot_count, dtype=jnp.int32)[None, :] < edge_counts[0])
        .astype(jnp.float32)
        .reshape(-1)
    )
    measured = measured.reshape(3, -1)
    confidence = confidence.reshape(3, -1)
    rotation = rotations(rot_vector.reshape(3, -1))
    diagonal = jnp.stack(
        [anchor if first_c == second_c else jnp.zeros_like(anchor) for first_c, second_c in PAIRS]
    )

    def window_of(field):
        window = field
        width = 1
        while width < pair_count:
            ahead = shifted(window, "blk", -width)
            window = jnp.concatenate([window, ahead], axis=1)
            width = width * 2
        return window

    def returned(far_sums):
        current = far_sums
        width = pair_count
        while width > 1:
            half_width = width // 2
            moved = shifted(current[:, half_width:width], "blk", half_width)
            current = current[:, :half_width] + moved
            width = half_width
        return current[:, 0]

    def reduce_halves(sums):
        return gathered_total(sums, "rep")

    def collect(far_terms, near_terms):
        channels = far_terms.shape[0]
        far_sums = spread(far_terms, second, window_span).reshape(channels, pair_count, tile_cams)
        near_sums = spread(near_terms, first, tile_cams)
        return reduce_halves(returned(far_sums) + near_sums)

    def precond_sum(residual, scaled):
        return taken_together(jnp.sum(residual * scaled), "blk")

    estimate = start_angles
    weights = live
    for sweep_index in range(PASSES):
        window = window_of(estimate)
        misfit = measured - (window[:, second] - rotate(rotation, estimate[:, first]))
        weights = live / jnp.sqrt(jnp.sum(confidence * misfit * misfit, axis=0) + SOFTEN * SOFTEN)
        weighted = weights * confidence
        terms = weighted * misfit
        far_part, near_part = block_parts(weighted, rotation)
        near_terms = jnp.concatenate([-rotate_back(rotation, terms), near_part], axis=0)
        far_terms = jnp.concatenate([terms, far_part], axis=0)
        totals = collect(far_terms, near_terms)
        residual = totals[:3] - anchor * estimate
        blocks = totals[3:] + diagonal
        scaled = inverse_apply(blocks, residual)
        direction = scaled
        norm_now = precond_sum(residual, scaled)
        for inner_index in range(ITERS):
            window = window_of(direction)
            changed = window[:, second] - rotate(rotation, direction[:, first])
            pushed = weighted * changed
            image = collect(pushed, -rotate_back(rotation, pushed)) + anchor * direction
            step_size = norm_now / taken_together(jnp.sum(direction * image), "blk")
            estimate = estimate + step_size * direction
            residual = residual - step_size * image
            if inner_index + 1 < ITERS:
                scaled = inverse_apply(blocks, residual)
                norm_next = precond_sum(residual, scaled)
                direction = scaled + norm_next / norm_now * direction
                norm_now = norm_next
    return (estimate, weights.reshape(1, pair_count, slot_count))


def solution(mesh):
    return jax.shard_map(
        on_device,
        mesh=mesh,
        in_specs=(
            P(None, "blk", None, "rep"),
            P(None, "blk", None, "rep"),
            P(None, "blk", None, "rep"),
            P("blk", None, "rep"),
            P("blk", None, "rep"),
            P("blk", None, "rep"),
            P(None, "blk"),
            P("blk"),
        ),
        out_specs=(P(None, "blk"), P("blk", None, "rep")),
        check_vma=False,
    )
```

profile of v0, /device:TPU:1, one launch (start us, length us, event | category | flops | bytes accessed | tf_op | source)
XLA Modules:
  0.0 1439.9 jit_solution(12092659010590915237)
XLA Ops:
  5.9 17.3 %gather_fusion.1 = f32[6144,3]{1,0:T(8,128)S(1)} fusion(f32[3,2048]{0,1:T(8,128)} %copy.1059, s32[6144]{0:T(1024)S(1)} %broadcast_clamp_fusion), kind=kCustom, calls=%fused_computation.1 | custom fusion | bytes 172032 | tf_op jit(solution)/shard_map/gather | solution.py:164
  59.8 24.3 %gather_fusion = f32[6144,3]{1,0:T(8,128)} fusion(f32[3,16384]{0,1:T(8,128)} %copy.1058, s32[6144]{0:T(1024)S(1)} %broadcast_clamp_fusion.1), kind=kCustom, calls=%fused_computation | custom fusion | bytes 172032 | tf_op jit(solution)/shard_map/gather | solution.py:164
  91.5 9.5 fusion.12
  127.6 37.4 %scatter_custom_fusion = f32[9,16384]{0,1:T(8,128)} fusion(s32[6144]{0:T(1024)} %bitcast.247, f32[6144,9]{1,0:T(8,128)} %copy.1069, f32[]{:T(128)} %constant.7.clone.1), kind=kCustom, calls=%fused_computation.39 | custom fusion | flops 55296 | bytes 590336 | tf_op jit(solution)/shard_map/vmap()/scatter-add | solution.py:103
  215.8 32.3 %scatter_fusion = f32[9,2048]{0,1:T(8,128)} fusion(f32[9,2048]{0,1:T(8,128)} %bitcast.197, s32[6144]{0:T(1024)S(1)} %reshape.837, f32[6144,9]{1,0:T(8,128)} %copy.1077), kind=kCustom, calls=%fused_computation.13 | custom fusion | flops 55296 | bytes 688128 | tf_op jit(solution)/shard_map/vmap()/scatter-add | solution.py:103
  278.4 22.1 %gather_fusion.3 = f32[6144,3]{1,0:T(8,128)} fusion(f32[3,2048]{0,1:T(8,128)} %copy.1081, s32[6144]{0:T(1024)S(1)} %broadcast_clamp_fusion), kind=kCustom, calls=%fused_computation.3 | custom fusion | bytes 172032 | tf_op jit(solution)/shard_map/gather | solution.py:179
  318.0 24.3 %gather_fusion.2 = f32[6144,3]{1,0:T(8,128)} fusion(f32[3,16384]{0,1:T(8,128)} %copy.1080, s32[6144]{0:T(1024)S(1)} %broadcast_clamp_fusion.1), kind=kCustom, calls=%fused_computation.2 | custom fusion | bytes 172032 | tf_op jit(solution)/shard_map/gather | solution.py:179
  347.2 34.2 %scatter_custom_fusion.2 = f32[3,16384]{0,1:T(8,128)} fusion(s32[6144]{0:T(1024)} %bitcast.248, f32[]{:T(128)} %constant.7.clone.1, f32[3,6144]{0,1:T(8,128)} %fusion.21), kind=kCustom, calls=%fused_computation.35 | custom fusion | flops 18432 | bytes 3342848 | tf_op jit(solution)/shard_map/vmap()/scatter-add | solution.py:103
  417.9 32.3 %scatter_fusion.1 = f32[3,2048]{0,1:T(8,128)} fusion(f32[3,2048]{0,1:T(8,128)} %bitcast.203, s32[6144]{0:T(1024)S(1)} %reshape.837, f32[6144,3]{1,0:T(8,128)} %copy.1088), kind=kCustom, calls=%fused_computation.15 | custom fusion | flops 18432 | bytes 245760 | tf_op jit(solution)/shard_map/vmap()/scatter-add | solution.py:103
  461.7 14.3 all_to_all.48
  497.1 12.8 all_to_all.49
  525.1 22.1 %gather_fusion.5 = f32[6144,3]{1,0:T(8,128)} fusion(f32[3,2048]{0,1:T(8,128)} %copy.1092, s32[6144]{0:T(1024)S(1)} %broadcast_clamp_fusion), kind=kCustom, calls=%fused_computation.5 | custom fusion | bytes 172032 | tf_op jit(solution)/shard_map/gather | solution.py:179
  573.0 24.3 %gather_fusion.4 = f32[6144,3]{1,0:T(8,128)} fusion(f32[3,16384]{0,1:T(8,128)} %pad_maximum_fusion, s32[6144]{0:T(1024)S(1)} %broadcast_clamp_fusion.1), kind=kCustom, calls=%fused_computation.4 | custom fusion | bytes 172032 | tf_op jit(solution)/shard_map/gather | solution.py:179
  602.3 34.2 %scatter_custom_fusion.4 = f32[3,16384]{0,1:T(8,128)} fusion(s32[6144]{0:T(1024)} %bitcast.249, f32[]{:T(128)} %constant.7.clone.1, f32[3,6144]{0,1:T(8,128)} %fusion.19), kind=kCustom, calls=%fused_computation.33 | custom fusion | flops 18432 | bytes 3342848 | tf_op jit(solution)/shard_map/vmap()/scatter-add | solution.py:103
  667.0 33.9 %scatter_fusion.2 = f32[3,2048]{0,1:T(8,128)S(1)} fusion(f32[3,2048]{0,1:T(8,128)S(1)} %bitcast.205, s32[6144]{0:T(1024)S(1)} %reshape.837, f32[6144,3]{1,0:T(8,128)} %copy.1103), kind=kCustom, calls=%fused_computation.17 | custom fusion | flops 18432 | bytes 245760 | tf_op jit(solution)/shard_map/vmap()/scatter-add | solution.py:103
  707.5 17.1 %all_to_all.50 = f32[64,1,1]{2,1,0:T(1,128)S(1)} all-to-all(f32[64,1,1]{2,1,0:T(1,128)S(1)} %broadcast_in_dim.22), channel_id=1, replica_groups=mesh['blk'=64,'rep'=2] {'blk'}, dimensions={0} | all-to-all | bytes 512 | tf_op jit(solution)/shard_map/all_to_all | solution.py:27
  736.1 20.9 %gather_fusion.7 = f32[6144,3]{1,0:T(8,128)} fusion(f32[3,2048]{0,1:T(8,128)S(1)} %copy.1106, s32[6144]{0:T(1024)S(1)} %broadcast_clamp_fusion), kind=kCustom, calls=%fused_computation.7 | custom fusion | bytes 172032 | tf_op jit(solution)/shard_map/gather | solution.py:164
  778.4 24.3 %gather_fusion.6 = f32[6144,3]{1,0:T(8,128)} fusion(f32[3,16384]{0,1:T(8,128)} %pad_maximum_fusion.1, s32[6144]{0:T(1024)S(1)} %broadcast_clamp_fusion.1), kind=kCustom, calls=%fused_computation.6 | custom fusion | bytes 172032 | tf_op jit(solution)/shard_map/gather | solution.py:164
  810.7 9.7 fusion.13
  846.1 37.2 %scatter_custom_fusion.6 = f32[9,16384]{0,1:T(8,128)} fusion(s32[6144]{0:T(1024)} %bitcast.250, f32[6144,9]{1,0:T(8,128)} %copy.1118, f32[]{:T(128)} %constant.7.clone.1), kind=kCustom, calls=%fused_computation.37 | custom fusion | flops 55296 | bytes 590336 | tf_op jit(solution)/shard_map/vmap()/scatter-add | solution.py:103
  927.8 32.3 %scatter_fusion.3 = f32[9,2048]{0,1:T(8,128)} fusion(f32[9,2048]{0,1:T(8,128)} %bitcast.199, s32[6144]{0:T(1024)S(1)} %reshape.837, f32[6144,9]{1,0:T(8,128)} %copy.1123), kind=kCustom, calls=%fused_computation.19 | custom fusion | flops 55296 | bytes 688128 | tf_op jit(solution)/shard_map/vmap()/scatter-add | solution.py:103
  989.0 22.1 %gather_fusion.9 = f32[6144,3]{1,0:T(8,128)} fusion(f32[3,2048]{0,1:T(8,128)} %copy.1127, s32[6144]{0:T(1024)S(1)} %broadcast_clamp_fusion), kind=kCustom, calls=%fused_computation.9 | custom fusion | bytes 172032 | tf_op jit(solution)/shard_map/gather | solution.py:179
  1028.6 24.3 %gather_fusion.8 = f32[6144,3]{1,0:T(8,128)} fusion(f32[3,16384]{0,1:T(8,128)} %copy.1126, s32[6144]{0:T(1024)S(1)} %broadcast_clamp_fusion.1), kind=kCustom, calls=%fused_computation.8 | custom fusion | bytes 172032 | tf_op jit(solution)/shard_map/gather | solution.py:179
  1057.8 34.2 %scatter_custom_fusion.8 = f32[3,16384]{0,1:T(8,128)} fusion(s32[6144]{0:T(1024)} %bitcast.251, f32[]{:T(128)} %constant.7.clone.1, f32[3,6144]{0,1:T(8,128)} %fusion.17), kind=kCustom, calls=%fused_computation.31 | custom fusion | flops 18432 | bytes 3342848 | tf_op jit(solution)/shard_map/vmap()/scatter-add | solution.py:103
  1128.2 32.3 %scatter_fusion.4 = f32[3,2048]{0,1:T(8,128)} fusion(f32[3,2048]{0,1:T(8,128)} %bitcast.207, s32[6144]{0:T(1024)S(1)} %reshape.837, f32[6144,3]{1,0:T(8,128)} %copy.1134), kind=kCustom, calls=%fused_computation.21 | custom fusion | flops 18432 | bytes 245760 | tf_op jit(solution)/shard_map/vmap()/scatter-add | solution.py:103
  1172.0 14.4 all_to_all.51
  1208.0 12.6 all_to_all.52
  1236.1 22.1 %gather_fusion.11 = f32[6144,3]{1,0:T(8,128)} fusion(f32[3,2048]{0,1:T(8,128)} %copy.1138, s32[6144]{0:T(1024)S(1)} %broadcast_clamp_fusion), kind=kCustom, calls=%fused_computation.11 | custom fusion | bytes 172032 | tf_op jit(solution)/shard_map/gather | solution.py:179
  1284.0 24.3 %gather_fusion.10 = f32[6144,3]{1,0:T(8,128)} fusion(f32[3,16384]{0,1:T(8,128)} %pad_maximum_fusion.2, s32[6144]{0:T(1024)S(1)} %broadcast_clamp_fusion.1), kind=kCustom, calls=%fused_computation.10 | custom fusion | bytes 172032 | tf_op jit(solution)/shard_map/gather | solution.py:179
  1313.2 34.2 %scatter_custom_fusion.10 = f32[3,16384]{0,1:T(8,128)} fusion(s32[6144]{0:T(1024)} %bitcast.252, f32[]{:T(128)} %constant.7.clone.1, f32[3,6144]{0,1:T(8,128)} %fusion.15), kind=kCustom, calls=%fused_computation.29 | custom fusion | flops 18432 | bytes 3342848 | tf_op jit(solution)/shard_map/vmap()/scatter-add | solution.py:103
  1377.9 33.9 %scatter_fusion.5 = f32[3,2048]{0,1:T(8,128)S(1)} fusion(f32[3,2048]{0,1:T(8,128)S(1)} %bitcast.201, s32[6144]{0:T(1024)S(1)} %reshape.837, f32[6144,3]{1,0:T(8,128)} %copy.1149), kind=kCustom, calls=%fused_computation.23 | custom fusion | flops 18432 | bytes 245760 | tf_op jit(solution)/shard_map/vmap()/scatter-add | solution.py:103
  1419.1 9.9 all-to-all-start.7
  (479 shorter events, 648.8 us)
Async XLA Ops:
  0.6 27.1 %collective-permute-start = (f32[3,2048]{1,0:T(4,128)}, f32[3,2048]{1,0:T(4,128)}, u32[]{:S(2)}, u32[]{:S(2)}) collective-permute-start(f32[3,2048]{1,0:T(4,128)} %param.14), channel_id=1, source_target_pairs={{0,126},{2,0},{4,2},{6,4},{8,6},{10,8},{12,10},{14,12},{16,14},{18... | collective-permute-start | bytes 73736 | tf_op jit(solution)/shard_map/ppermute | solution.py:18
  28.5 8.5 collective-permute-start.1
  37.7 16.2 %collective-permute-start.2 = (f32[3,8192]{1,0:T(4,128)S(1)}, f32[3,8192]{1,0:T(4,128)S(1)}, u32[]{:S(2)}, u32[]{:S(2)}) collective-permute-start(f32[3,8192]{1,0:T(4,128)S(1)} %pad_maximum_fusion.7), channel_id=1, source_target_pairs={{0,120},{2,122},{4,124},{6,126},{8,0},{10,2},{12,4},{14,6},{16,8},... | collective-permute-start | bytes 294920 | tf_op jit(solution)/shard_map/ppermute | solution.py:18
  175.9 12.2 collective-permute-start.3
  190.0 8.5 collective-permute-start.4
  201.0 10.9 collective-permute-start.5
  267.6 35.8 %collective-permute-start.7 = (f32[3,4096]{1,0:T(4,128)}, f32[3,4096]{1,0:T(4,128)}, u32[]{:S(2)}, u32[]{:S(2)}) collective-permute-start(f32[3,4096]{1,0:T(4,128)} %pad_maximum_fusion.14), channel_id=1, source_target_pairs={{0,124},{2,126},{4,0},{6,2},{8,4},{10,6},{12,8},{14,10},{16,12},{1... | collective-permute-start | bytes 147464 | tf_op jit(solution)/shard_map/ppermute | solution.py:18
  305.0 5.6 collective-permute-start.8
  392.2 8.9 collective-permute-start.9
  402.2 7.2 collective-permute-start.10
  410.7 3.6 collective-permute-start.11
  477.2 13.0 all-to-all-start
  517.5 32.7 %collective-permute-start.13 = (f32[3,4096]{1,0:T(4,128)}, f32[3,4096]{1,0:T(4,128)}, u32[]{:S(2)}, u32[]{:S(2)}) collective-permute-start(f32[3,4096]{1,0:T(4,128)} %pad_maximum_fusion.15), channel_id=1, source_target_pairs={{0,124},{2,126},{4,0},{6,2},{8,4},{10,6},{12,8},{14,10},{16,12},{1... | collective-permute-start | bytes 147464 | tf_op jit(solution)/shard_map/ppermute | solution.py:18
  551.7 9.7 collective-permute-start.14
  647.4 8.5 collective-permute-start.15
  656.9 7.2 collective-permute-start.16
  730.1 29.3 %collective-permute-start.19 = (f32[3,4096]{1,0:T(4,128)S(1)}, f32[3,4096]{1,0:T(4,128)S(1)}, u32[]{:S(2)}, u32[]{:S(2)}) collective-permute-start(f32[3,4096]{1,0:T(4,128)S(1)} %pad_maximum_fusion.16), channel_id=1, source_target_pairs={{0,124},{2,126},{4,0},{6,2},{8,4},{10,6},{12,8},{14,10},{16,12},{1... | collective-permute-start | bytes 147464 | tf_op jit(solution)/shard_map/ppermute | solution.py:18
  760.1 6.0 collective-permute-start.20
  894.2 11.2 collective-permute-start.21
  906.6 8.6 collective-permute-start.22
  916.6 7.3 collective-permute-start.23
  979.0 35.0 %collective-permute-start.25 = (f32[3,4096]{1,0:T(4,128)}, f32[3,4096]{1,0:T(4,128)}, u32[]{:S(2)}, u32[]{:S(2)}) collective-permute-start(f32[3,4096]{1,0:T(4,128)} %pad_maximum_fusion.17), channel_id=1, source_target_pairs={{0,124},{2,126},{4,0},{6,2},{8,4},{10,6},{12,8},{14,10},{16,12},{1... | collective-permute-start | bytes 147464 | tf_op jit(solution)/shard_map/ppermute | solution.py:18
  1015.6 5.6 collective-permute-start.26
  1102.9 8.7 collective-permute-start.27
  1112.6 7.2 collective-permute-start.28
  1121.1 3.6 collective-permute-start.29
  1187.7 13.4 all-to-all-start.4
  1228.4 32.7 %collective-permute-start.31 = (f32[3,4096]{1,0:T(4,128)}, f32[3,4096]{1,0:T(4,128)}, u32[]{:S(2)}, u32[]{:S(2)}) collective-permute-start(f32[3,4096]{1,0:T(4,128)} %pad_maximum_fusion.18), channel_id=1, source_target_pairs={{0,124},{2,126},{4,0},{6,2},{8,4},{10,6},{12,8},{14,10},{16,12},{1... | collective-permute-start | bytes 147464 | tf_op jit(solution)/shard_map/ppermute | solution.py:18
  1262.7 9.7 collective-permute-start.32
  1358.4 8.4 collective-permute-start.33
  1367.8 7.2 collective-permute-start.34
  1419.1 17.8 %all-to-all-start.7 = ((f32[64,1,1]{2,1,0:T(1,128)}), f32[64,1,1]{2,1,0:T(1,128)S(1)}, u32[]{:S(2)}, u32[]{:S(2)}) async-start(f32[64,1,1]{2,1,0:T(1,128)} %broadcast_in_dim.26), calls=%async_computation.7 | async-start | bytes 65536 | tf_op jit(solution)/shard_map/all_to_all | solution.py:27
  (81 other events, 1007.4 us)
where the time goes:
time: 1450 us; the launch traced here: 1440 us
  local copies, waits for them, and re-layouts  577 us (40%)
  other arithmetic  568 us (39%)
  blocking collectives  109 us (8%)
  starting transfers between devices  92.8 us (6%)
  waiting for transfers between devices  84.1 us (6%)
    scatter-add x12, other arithmetic, spread(): jax.ops.segment_sum(values, index, num_segments=total)  408 us
    gather x12, local copies, waits for them, and re-layouts, on_device(): changed = window[:, second] - rotate(rotation, direction[:, first])  197 us
    ppermute x36, starting transfers between devices, shifted(): return lax.ppermute(value, axis, pairs)  72.2 us
    all_to_all x5, blocking collectives, from_everyone(): lax.all_to_all(jnp.broadcast_to(array[None], (peers, *array.shape)), axis...  71.2 us
    unnamed x180, local copies, waits for them, and re-layouts  69.8 us
    ppermute x36, waiting for transfers between devices, shifted(): return lax.ppermute(value, axis, pairs)  64.1 us
    gather x2, local copies, waits for them, and re-layouts, on_device(): window[:, second] - rotate(rotation, estimate[:, first])  48.6 us
    slice x18, local copies, waits for them, and re-layouts, returned(): moved = shifted(current[:, half_width:width], 'blk', half_width)  47.8 us
  transfers between devices with their start and end apart: 39, of which 22 were waited for; matrix products, arithmetic and copies ran while one was open for 19% of the time, Pallas kernels for 0%

commit v1 on v0

v1 whole, which is shorter than its diff:
```python
import functools

import jax
import jax.numpy as jnp
from jax import lax
from jax.experimental import pallas as pl
from jax.experimental.pallas import tpu as pltpu
from jax.sharding import PartitionSpec as P

PASSES = 2
SOFTEN = 0.05
MESH = pl.DeviceIdType.MESH
LANES = 128
HI = 8
GROUP = 8
PAIRS = ((0, 0), (0, 1), (0, 2), (1, 1), (1, 2), (2, 2))
F32 = jnp.float32
BF16 = jnp.bfloat16


def dot_nn(a, b):
    return lax.dot_general(a, b, (((1,), (0,)), ((), ())), preferred_element_type=F32)


def dot_nt(a, b):
    return lax.dot_general(a, b, (((1,), (1,)), ((), ())), preferred_element_type=F32)


def two_pieces(value):
    high = value.astype(BF16).astype(F32)
    return high, value - high


def kernel(
    n_blk,
    n_rep,
    measured_ref,
    rot_ref,
    conf_ref,
    first_ref,
    second_ref,
    counts_ref,
    start_ref,
    anchor_ref,
    est_out,
    weights_out,
    hot,
    himask,
    idx,
    rotm,
    meas,
    conf,
    live,
    wout,
    mis,
    wconf,
    chz,
    chu,
    send1,
    recv1,
    send2,
    recv2,
    est,
    halo,
    anc,
    inv,
    fz,
    fu,
    fr,
    fq,
    bsend,
    brecv,
    dsend,
    drecv,
    xsend,
    xrecv,
    g1send,
    g1recv,
    g2send,
    g2recv,
    lhs,
    s_init,
    r_init,
    s_b,
    r_b,
    s_d,
    r_d,
    s_x,
    r_x,
    s_g1,
    r_g1,
    s_g2,
    r_g2,
):
    pairs = idx.shape[0] // 3
    tiles = idx.shape[1]
    lo_count = est.shape[2]
    outer = n_blk // GROUP
    wide = outer * n_rep
    b = lax.axis_index("blk")
    r = lax.axis_index("rep")
    low = lax.rem(b, GROUP)
    high = b // GROUP
    mine2 = high * n_rep + r

    def ahead(k):
        return lax.rem(b + k, n_blk)

    def behind(k):
        return lax.rem(b + n_blk - k, n_blk)

    def copy(src, dst, send, recv, blk, rep):
        return pltpu.make_async_remote_copy(
            src_ref=src,
            dst_ref=dst,
            send_sem=send,
            recv_sem=recv,
            device_id={"blk": blk, "rep": rep},
            device_id_type=MESH,
        )

    barrier = pltpu.get_barrier_semaphore()

    def greet(blk, rep):
        pl.semaphore_signal(barrier, inc=1, device_id={"blk": blk, "rep": rep}, device_id_type=MESH)

    def greet_pairs(k, _):
        greet(ahead(k), r)
        greet(behind(k), r)
        return 0

    lax.fori_loop(1, pairs, greet_pairs, 0)
    greet(b, 1 - r)

    def inner_peer(j):
        return high * GROUP + lax.rem(low + j, GROUP)

    def outer_peer(j):
        other = lax.rem(mine2 + j, wide)
        return (other // n_rep) * GROUP + low, lax.rem(other, n_rep)

    def greet_inner(j, _):
        greet(inner_peer(j), r)
        return 0

    def greet_outer(j, _):
        blk, rep = outer_peer(j)
        greet(blk, rep)
        return 0

    lax.fori_loop(1, GROUP, greet_inner, 0)
    lax.fori_loop(1, wide, greet_outer, 0)

    def lanes_of(t):
        return pl.ds(t * LANES, LANES)

    live_all = lax.broadcasted_iota(jnp.int32, first_ref.shape[1:], 1) < counts_ref[0]
    live_all = jnp.where(live_all, 1.0, 0.0).astype(F32)
    for k in range(pairs):
        for t in range(tiles):
            at = slice(t * LANES, (t + 1) * LANES)
            live[k, t : t + 1] = live_all[k : k + 1, at]
            idx[k, t : t + 1] = first_ref[0, k : k + 1, at]
            idx[2 * pairs + k, t : t + 1] = second_ref[0, k : k + 1, at]
            for c in range(3):
                conf[k, c, t : t + 1] = conf_ref[c, 0, k : k + 1, at] * live_all[k : k + 1, at]
                meas[k, c, t : t + 1] = measured_ref[c, 0, k : k + 1, at]
                rotm[k, c, t : t + 1] = rot_ref[c, 0, k : k + 1, at]
    for h in range(HI):
        at = slice(h * lo_count, (h + 1) * lo_count)
        anc[h : h + 1] = anchor_ref[0:1, at]
        for c in range(3):
            est[c, h : h + 1] = start_ref[c : c + 1, at]

    def stage1(k, _):
        for c in range(3):
            send1[k, c] = conf[k, c]
        send1[k, 3] = idx[2 * pairs + k].astype(F32)
        return 0

    lax.fori_loop(0, pairs, stage1, 0)
    halo[0] = est[...]

    pl.semaphore_wait(barrier, 2 * (pairs - 1) + 1 + (GROUP - 1) + (wide - 1))

    def send_init(k):
        return copy(send1.at[k], recv1.at[k], s_init.at[0, k], r_init.at[0, k], ahead(k), r)

    def send_mis(k):
        return copy(send2.at[k], recv2.at[k], s_init.at[1, k], r_init.at[1, k], ahead(k), r)

    def send_halo(k):
        return copy(halo.at[0], halo.at[k], s_init.at[2, k], r_init.at[2, k], behind(k), r)

    def start_init(k, _):
        send_init(k).start()
        send_halo(k).start()
        return 0

    lax.fori_loop(1, pairs, start_init, 0)
    recv1[0] = send1[0]

    def rotations(k, _):
        v = [rotm[k, c] for c in range(3)]
        squared = v[0] * v[0] + v[1] * v[1] + v[2] * v[2]
        factor = 2.0 / (1.0 + squared)
        zero = jnp.zeros_like(squared)
        skew = ((zero, -v[2], v[1]), (v[2], zero, -v[0]), (-v[1], v[0], zero))
        for i in range(3):
            for j in range(3):
                term = skew[i][j] + v[i] * v[j]
                if i == j:
                    rotm[k, 3 * i + j] = 1.0 + factor * (term - squared)
                else:
                    rotm[k, 3 * i + j] = factor * term
        return 0

    lax.fori_loop(0, pairs, rotations, 0)

    def build(g):
        for t in range(tiles):
            where = idx[g, t : t + 1]
            low_part = lax.rem(where, lo_count)
            high_part = where // lo_count
            at = slice(t * LANES, (t + 1) * LANES)
            himask[g, :, at] = jnp.where(
                lax.broadcasted_iota(jnp.int32, (HI, LANES), 0) == high_part, 1.0, 0.0
            ).astype(F32)
            hot[g, :, at] = jnp.where(
                lax.broadcasted_iota(jnp.int32, (lo_count, LANES), 0) == low_part, 1.0, 0.0
            ).astype(BF16)

    def build_near(k, _):
        build(k)
        return 0

    def build_second(k, _):
        build(2 * pairs + k)
        return 0

    def table_of(field):
        rows = []
        for c in range(3):
            rows.extend(two_pieces(field[c]))
        return jnp.concatenate(rows, axis=0).astype(BF16)

    def gather(table, g):
        full = dot_nn(table, hot[g])
        mask = himask[g]
        found = []
        for c in range(3):
            part = (full[16 * c : 16 * c + 8] + full[16 * c + 8 : 16 * c + 16]) * mask
            row = jnp.sum(part, axis=0, keepdims=True)
            found.append(
                jnp.concatenate([row[:, t * LANES : (t + 1) * LANES] for t in range(tiles)], axis=0)
            )
        return found

    def rotate(k, vec):
        return [
            rotm[k, 3 * i] * vec[0] + rotm[k, 3 * i + 1] * vec[1] + rotm[k, 3 * i + 2] * vec[2]
            for i in range(3)
        ]

    def rotate_back(k, vec):
        return [
            rotm[k, i] * vec[0] + rotm[k, 3 + i] * vec[1] + rotm[k, 6 + i] * vec[2]
            for i in range(3)
        ]

    lax.fori_loop(0, pairs, build_near, 0)
    table = table_of(est)

    def near_start(i, _):
        k = lax.rem(i + 1, pairs)
        turned = rotate(k, gather(table, k))
        for c in range(3):
            send2[k, c] = meas[k, c] + turned[c]

        @pl.when(k != 0)
        def _():
            send_mis(k).start()

        return 0

    lax.fori_loop(0, pairs, near_start, 0)
    recv2[0] = send2[0]

    lax.fori_loop(0, pairs, build_second, 0)

    def wait_halo(k, _):
        copy(halo.at[0], halo.at[k], s_init.at[2, k], r_init.at[2, k], b, r).wait_recv()
        return 0

    lax.fori_loop(1, pairs, wait_halo, 0)

    def own_misfit(k, _):
        there = gather(table_of(halo.at[k]), 2 * pairs + k)
        for c in range(3):
            mis[0, k, c] = send2[k, c] - there[c]
        return 0

    lax.fori_loop(0, pairs, own_misfit, 0)

    def wait_init(k, _):
        copy(send1.at[k], recv1.at[k], s_init.at[0, k], r_init.at[0, k], b, r).wait_recv()
        return 0

    lax.fori_loop(1, pairs, wait_init, 0)

    def build_far(k, _):
        idx[pairs + k] = recv1[k, 3].astype(jnp.int32)
        build(pairs + k)
        return 0

    lax.fori_loop(0, pairs, build_far, 0)

    def wait_mis(k, _):
        copy(send2.at[k], recv2.at[k], s_init.at[1, k], r_init.at[1, k], b, r).wait_recv()
        return 0

    lax.fori_loop(1, pairs, wait_mis, 0)

    def far_misfit(k, _):
        there = gather(table, pairs + k)
        for c in range(3):
            mis[1, k, c] = recv2[k, c] - there[c]
        return 0

    lax.fori_loop(0, pairs, far_misfit, 0)

    def put(slot, at_row, terms, g):
        for n, term in enumerate(terms):
            head, tail = two_pieces(term)
            for t in range(tiles):
                at = slice(t * LANES, (t + 1) * LANES)
                mask = himask[g, :, at]
                both = jnp.concatenate([head[t : t + 1] * mask, tail[t : t + 1] * mask], axis=0)
                lhs[slot, at_row + 16 * n : at_row + 16 * n + 16, at] = both.astype(BF16)

    def summed(totals, channel):
        return totals[16 * channel : 16 * channel + 8] + totals[16 * channel + 8 : 16 * channel + 16]

    def full_sum(value):
        return jnp.sum(jnp.sum(value, axis=0, keepdims=True), axis=1, keepdims=True)

    def invert(vec_ref, out_ref):
        for i in range(3):
            look = ((0, 1, 2), (1, 3, 4), (2, 4, 5))[i]
            out_ref[i] = (
                inv[look[0]] * vec_ref[0] + inv[look[1]] * vec_ref[1] + inv[look[2]] * vec_ref[2]
            )

    def exchange_start(x, table):
        def step(i, _):
            k = lax.rem(i + 1, pairs)
            turned = rotate(k, gather(table, k))
            there = gather(table, pairs + k)
            for c in range(3):
                xsend[x, 0, k, c] = turned[c]
                xsend[x, 1, k, c] = there[c]

            @pl.when(k != 0)
            def _():
                send_back(x, k).start()
                send_ahead(x, k).start()

            return 0

        lax.fori_loop(0, pairs, step, 0)
        xrecv[x, 0, 0] = xsend[x, 0, 0]
        xrecv[x, 1, 0] = xsend[x, 1, 0]

    def send_ahead(x, k):
        return copy(xsend.at[x, 0, k], xrecv.at[x, 0, k], s_x.at[x, 0, k], r_x.at[x, 0, k], ahead(k), r)

    def send_back(x, k):
        return copy(xsend.at[x, 1, k], xrecv.at[x, 1, k], s_x.at[x, 1, k], r_x.at[x, 1, k], behind(k), r)

    def wait_exchange(x, k):
        @pl.when(k != 0)
        def _():
            copy(xsend.at[x, 1, k], xrecv.at[x, 1, k], s_x.at[x, 1, k], r_x.at[x, 1, k], b, r).wait_recv()
            copy(xsend.at[x, 0, k], xrecv.at[x, 0, k], s_x.at[x, 0, k], r_x.at[x, 0, k], b, r).wait_recv()

    lane = lax.broadcasted_iota(jnp.int32, (1, LANES), 1)

    for p in range(PASSES):
        def near_sums(k, totals):
            m = [mis[0, k, c] for c in range(3)]
            cf = [conf[k, c] for c in range(3)]
            squares = cf[0] * m[0] * m[0] + cf[1] * m[1] * m[1] + cf[2] * m[2] * m[2]
            weight = live[k] / jnp.sqrt(squares + SOFTEN * SOFTEN)
            wout[k] = weight
            wc = [weight * cf[c] for c in range(3)]
            for c in range(3):
                wconf[0, k, c] = wc[c]
            back = rotate_back(k, [wc[c] * m[c] for c in range(3)])
            rot = [[rotm[k, 3 * i + j] for j in range(3)] for i in range(3)]
            terms = [-value for value in back]
            for f, s in PAIRS:
                terms.append(
                    rot[0][f] * wc[0] * rot[0][s]
                    + rot[1][f] * wc[1] * rot[1][s]
                    + rot[2][f] * wc[2] * rot[2][s]
                )
            put(0, 0, terms, k)
            return totals + dot_nt(lhs[0], hot[k])

        def far_sums(k, totals):
            m = [mis[1, k, c] for c in range(3)]
            cf = [recv1[k, c] for c in range(3)]
            squares = cf[0] * m[0] * m[0] + cf[1] * m[1] * m[1] + cf[2] * m[2] * m[2]
            weight = 1.0 / jnp.sqrt(squares + SOFTEN * SOFTEN)
            wc = [weight * cf[c] for c in range(3)]
            for c in range(3):
                wconf[1, k, c] = wc[c]
            put(1, 0, [wc[c] * m[c] for c in range(3)] + wc, pairs + k)
            return totals + dot_nt(lhs[1, 0:96], hot[pairs + k])

        near = lax.fori_loop(0, pairs, near_sums, jnp.zeros((144, lo_count), F32))
        far = lax.fori_loop(0, pairs, far_sums, jnp.zeros((96, lo_count), F32))
        for n in range(9):
            total = summed(near, n)
            spot = {0: 0, 1: 1, 2: 2, 3: 3, 6: 4, 8: 5}.get(n)
            if spot is not None:
                total = total + summed(far, spot)
            bsend[p, n] = total
        copy(bsend.at[p], brecv.at[p], s_b.at[p], r_b.at[p], b, 1 - r).start()
        copy(bsend.at[p], brecv.at[p], s_b.at[p], r_b.at[p], b, 1 - r).wait_recv()
        anchor = anc[...]
        for c in range(3):
            fr[c] = bsend[p, c] + brecv[p, c] - anchor * est[c]
        blocks = []
        for n, (f, s) in enumerate(PAIRS):
            block = bsend[p, 3 + n] + brecv[p, 3 + n]
            blocks.append(block + anchor if f == s else block)
        adjugate = [
            blocks[3] * blocks[5] - blocks[4] * blocks[4],
            blocks[2] * blocks[4] - blocks[1] * blocks[5],
            blocks[1] * blocks[4] - blocks[2] * blocks[3],
            blocks[0] * blocks[5] - blocks[2] * blocks[2],
            blocks[1] * blocks[2] - blocks[0] * blocks[4],
            blocks[0] * blocks[3] - blocks[1] * blocks[1],
        ]
        determinant = blocks[0] * adjugate[0] + blocks[1] * adjugate[1] + blocks[2] * adjugate[2]
        for n in range(6):
            inv[n] = adjugate[n] / determinant
        invert(fr, fz)

        x = 2 * p
        exchange_start(x, table_of(fz))

        def product_near(k, totals):
            wait_exchange(x, k)
            change = [xrecv[x, 1, k, c] - xsend[x, 0, k, c] for c in range(3)]
            pushed = []
            square = totals[1]
            for c in range(3):
                chz[0, k, c] = change[c]
                pushed.append(wconf[0, k, c] * change[c])
                square = square + pushed[c] * change[c]
            put(0, 0, [-value for value in rotate_back(k, pushed)], k)
            return totals[0] + dot_nt(lhs[0, 0:48], hot[k]), square

        def product_far(k, totals):
            change = [xsend[x, 1, k, c] - xrecv[x, 0, k, c] for c in range(3)]
            pushed = []
            for c in range(3):
                chz[1, k, c] = change[c]
                pushed.append(wconf[1, k, c] * change[c])
            put(1, 0, pushed, pairs + k)
            return totals + dot_nt(lhs[1, 0:48], hot[pairs + k])

        zero_row = jnp.zeros((tiles, LANES), F32)
        totals, z_square = lax.fori_loop(
            0, pairs, product_near, (jnp.zeros((48, lo_count), F32), zero_row)
        )
        totals = lax.fori_loop(0, pairs, product_far, totals)
        for c in range(3):
            dsend[p, c] = summed(totals, c)
        copy(dsend.at[p], drecv.at[p], s_d.at[p], r_d.at[p], b, 1 - r).start()
        copy(dsend.at[p], drecv.at[p], s_d.at[p], r_d.at[p], b, 1 - r).wait_recv()
        for c in range(3):
            fq[c] = dsend[p, c] + drecv[p, c] + anchor * fz[c]
        invert(fq, fu)

        y = 2 * p + 1
        exchange_start(y, table_of(fu))

        def change_u(k, square):
            wait_exchange(y, k)
            for c in range(3):
                change = xrecv[y, 1, k, c] - xsend[y, 0, k, c]
                chu[0, k, c] = change
                square = square + wconf[0, k, c] * change * change
                chu[1, k, c] = xsend[y, 1, k, c] - xrecv[y, 0, k, c]
            return square

        u_square = lax.fori_loop(0, pairs, change_u, zero_row)

        half = 1.0 / n_rep
        rz = fr[0] * fz[0] + fr[1] * fz[1] + fr[2] * fz[2]
        zz = anchor * (fz[0] * fz[0] + fz[1] * fz[1] + fz[2] * fz[2])
        uu = anchor * (fu[0] * fu[0] + fu[1] * fu[1] + fu[2] * fu[2])
        uq = fu[0] * fq[0] + fu[1] * fq[1] + fu[2] * fq[2]
        parts = (
            half * full_sum(rz),
            half * full_sum(zz) + full_sum(z_square),
            half * full_sum(uq),
            half * full_sum(uu) + full_sum(u_square),
        )
        row = jnp.zeros((1, LANES), F32)
        for n, part in enumerate(parts):
            row = jnp.where(lane == n, part, row)

        def reduce_over(row, send_ref, recv_ref, s_sem, r_sem, count, me, peer):
            send_ref[p] = row

            def start(j, _):
                blk, rep = peer(j)
                copy(send_ref.at[p], recv_ref.at[p, me], s_sem.at[p, j], r_sem.at[p, me], blk, rep).start()
                return 0

            lax.fori_loop(1, count, start, 0)
            recv_ref[p, me] = row

            def wait(j, _):
                other = lax.rem(me + j, count)
                copy(send_ref.at[p], recv_ref.at[p, other], s_sem.at[p, j], r_sem.at[p, other], b, r).wait_recv()
                return 0

            lax.fori_loop(1, count, wait, 0)
            total = recv_ref[p, 0]
            for n in range(1, count):
                total = total + recv_ref[p, n]
            return total

        row = reduce_over(
            row, g1send, g1recv, s_g1, r_g1, GROUP, low, lambda j: (inner_peer(j), r)
        )
        row = reduce_over(row, g2send, g2recv, s_g2, r_g2, wide, mine2, outer_peer)

        def scalar(n):
            return jnp.sum(jnp.where(lane == n, row, 0.0), axis=1, keepdims=True)

        rz, zq, uq, uw = scalar(0), scalar(1), scalar(2), scalar(3)
        alpha = rz / zq
        norm_next = rz - 2.0 * alpha * zq + alpha * alpha * uq
        beta = norm_next / rz
        grown = 1.0 + beta
        along = grown * grown * zq - 2.0 * alpha * grown * uq + alpha * alpha * uw
        alpha_two = norm_next / along
        of_z = alpha + alpha_two * grown
        of_u = -alpha * alpha_two
        for c in range(3):
            est[c] = est[c] + of_z * fz[c] + of_u * fu[c]
        if p + 1 < PASSES:

            def new_misfit(k, _):
                for side in range(2):
                    for c in range(3):
                        mis[side, k, c] = (
                            mis[side, k, c] - of_z * chz[side, k, c] - of_u * chu[side, k, c]
                        )
                return 0

            lax.fori_loop(0, pairs, new_misfit, 0)

    for k in range(pairs):
        for t in range(tiles):
            weights_out[0, k : k + 1, t * LANES : (t + 1) * LANES] = wout[k, t : t + 1]
    for h in range(HI):
        at = slice(h * lo_count, (h + 1) * lo_count)
        for c in range(3):
            est_out[c : c + 1, at] = est[c, h : h + 1]

    def drain_init(k, _):
        send_init(k).wait_send()
        send_mis(k).wait_send()
        send_halo(k).wait_send()
        for x in range(2 * PASSES):
            send_ahead(x, k).wait_send()
            send_back(x, k).wait_send()
        return 0

    lax.fori_loop(1, pairs, drain_init, 0)
    for p in range(PASSES):
        copy(bsend.at[p], brecv.at[p], s_b.at[p], r_b.at[p], b, 1 - r).wait_send()
        copy(dsend.at[p], drecv.at[p], s_d.at[p], r_d.at[p], b, 1 - r).wait_send()
        for j in range(1, GROUP):
            copy(g1send.at[p], g1recv.at[p, 0], s_g1.at[p, j], r_g1.at[p, 0], b, r).wait_send()
        for j in range(1, wide):
            copy(g2send.at[p], g2recv.at[p, 0], s_g2.at[p, j], r_g2.at[p, 0], b, r).wait_send()


def on_device(
    n_blk,
    n_rep,
    measured,
    rot_vector,
    confidence,
    first_local,
    second_local,
    edge_counts,
    start_angles,
    anchor,
):
    pairs, slots = first_local.shape[1], first_local.shape[2]
    cams = start_angles.shape[1]
    tiles = slots // LANES
    lo = cams // HI
    wide = (n_blk // GROUP) * n_rep
    vmem = pltpu.VMEM
    sem = pltpu.SemaphoreType.DMA

    def edges(*lead):
        return vmem((*lead, tiles, LANES), F32)

    def cameras(*lead):
        return vmem((*lead, HI, lo), F32)

    scratch = [
        vmem((3 * pairs, lo, slots), BF16),
        vmem((3 * pairs, HI, slots), F32),
        vmem((3 * pairs, tiles, LANES), jnp.int32),
        edges(pairs, 9),
        edges(pairs, 3),
        edges(pairs, 3),
        edges(pairs),
        edges(pairs),
        edges(2, pairs, 3),
        edges(2, pairs, 3),
        edges(2, pairs, 3),
        edges(2, pairs, 3),
        edges(pairs, 4),
        edges(pairs, 4),
        edges(pairs, 3),
        edges(pairs, 3),
        cameras(3),
        cameras(pairs, 3),
        cameras(),
        cameras(6),
        cameras(3),
        cameras(3),
        cameras(3),
        cameras(3),
        cameras(PASSES, 9),
        cameras(PASSES, 9),
        cameras(PASSES, 3),
        cameras(PASSES, 3),
        edges(2 * PASSES, 2, pairs, 3),
        edges(2 * PASSES, 2, pairs, 3),
        vmem((PASSES, 1, LANES), F32),
        vmem((PASSES, GROUP, 1, LANES), F32),
        vmem((PASSES, 1, LANES), F32),
        vmem((PASSES, wide, 1, LANES), F32),
        vmem((2, 144, slots), BF16),
        sem((3, pairs)),
        sem((3, pairs)),
        sem((PASSES,)),
        sem((PASSES,)),
        sem((PASSES,)),
        sem((PASSES,)),
        sem((2 * PASSES, 2, pairs)),
        sem((2 * PASSES, 2, pairs)),
        sem((PASSES, GROUP)),
        sem((PASSES, GROUP)),
        sem((PASSES, wide)),
        sem((PASSES, wide)),
    ]
    whole = pl.BlockSpec(memory_space=pltpu.VMEM)
    return pl.pallas_call(
        functools.partial(kernel, n_blk, n_rep),
        out_shape=(
            jax.ShapeDtypeStruct((3, cams), F32),
            jax.ShapeDtypeStruct((1, pairs, slots), F32),
        ),
        in_specs=[whole] * 8,
        out_specs=(whole, whole),
        scratch_shapes=scratch,
        compiler_params=pltpu.CompilerParams(
            collective_id=0, has_side_effects=True, vmem_limit_bytes=60 * 1024 * 1024
        ),
    )(
        measured,
        rot_vector,
        confidence,
        first_local,
        second_local,
        edge_counts,
        start_angles,
        anchor.reshape(1, -1),
    )


def solution(mesh):
    return jax.shard_map(
        functools.partial(on_device, mesh.shape["blk"], mesh.shape["rep"]),
        mesh=mesh,
        in_specs=(
            P(None, "blk", None, "rep"),
            P(None, "blk", None, "rep"),
            P(None, "blk", None, "rep"),
            P("blk", None, "rep"),
            P("blk", None, "rep"),
            P("blk", None, "rep"),
            P(None, "blk"),
            P("blk"),
        ),
        out_specs=(P(None, "blk"), P("blk", None, "rep")),
        check_vma=False,
    )
```

time: 1450 us -> 101 us (0.07)
  local copies, waits for them, and re-layouts: 577 us -> 3.32 us
  other arithmetic: 568 us -> 0 us
  blocking collectives: 109 us -> 0 us
  Pallas kernels: 0 us -> 96.3 us
  starting transfers between devices: 92.8 us -> 0 us
  waiting for transfers between devices: 84.1 us -> 0 us
    scatter-add x12 -> x0, other arithmetic: 408 us -> none  [spread(): jax.ops.segment_sum(values, index, num_segments=total)]
    gather x18 -> x0, local copies, waits for them, and re-layouts: 288 us -> none  [the longest x12 197 us: on_device(): changed = window[:, second] - rotate(rotation, direction[:, first])]
    pallas_call x0 -> x1, Pallas kernels: none -> 96.3 us  [on_device(): pl.pallas_call(functools.partial(kernel, n_blk, n_rep), out_shape=(jax.Sh...]
    slice x27 -> x0, local copies, waits for them, and re-layouts: 76.3 us -> none  [the longest x18 47.8 us: returned(): moved = shifted(current[:, half_width:width], 'blk', half_width)]
    ppermute x36 -> x0, starting transfers between devices: 72.2 us -> none  [shifted(): return lax.ppermute(value, axis, pairs)]
    all_to_all x5 -> x0, blocking collectives: 71.2 us -> none  [from_everyone(): lax.all_to_all(jnp.broadcast_to(array[None], (peers, *array.shape)), axis...]
    unnamed x180 -> x7, local copies, waits for them, and re-layouts: 69.8 us -> 3.32 us
    ppermute x36 -> x0, waiting for transfers between devices: 64.1 us -> none  [shifted(): return lax.ppermute(value, axis, pairs)]
  transfers between devices with their start and end apart: 39 -> 0, of which waited for: 22 -> 0; matrix products, arithmetic and copies ran while one was open for 19% -> 0% of each run, Pallas kernels for 0% -> 0%
where the time goes in v1:
time: 101 us; the launch traced here: 100 us
  Pallas kernels  96.3 us (95%)
  local copies, waits for them, and re-layouts  3.32 us (3%)
    pallas_call x1, Pallas kernels, on_device(): pl.pallas_call(functools.partial(kernel, n_blk, n_rep), out_shape=(jax.Sh...  96.3 us
    unnamed x7, local copies, waits for them, and re-layouts  3.32 us

profile of v1, /device:TPU:1, one launch (start us, length us, event | category | flops | bytes accessed | tf_op | source)
XLA Modules:
  0.0 100.2 jit_solution(13540021825752801751)
XLA Ops:
  0.6 0.0 copy-start.1
  0.6 0.6 copy-done.1
  1.3 0.7 copy.10.counts_ref
  2.0 96.3 %shard_map.95 = (f32[3,2048]{1,0:T(4,128)}, f32[1,8,768]{2,1,0:T(8,128)}) custom-call(f32[3,1,8,768]{3,2,1,0:T(8,128)} %measured_ref.1, f32[3,1,8,768]{3,2,1,0:T(8,128)} %rot_ref.1, f32[3,1,8,768]{3,2,1,0:T(8,128)} %conf_ref.1, s32[1,8,768]{2,1,0:T(8,128)} %first_ref.1, s32[1,8,768]{2,1,0:T(8,128)} %second_ref.1, s32[1,8,1]{2,1,0:T(8,128)} %copy.10.counts_ref, ...), custom_call_target="tpu_custom_call" | custom-call | tf_op jit(solution)/shard_map/pallas_call | solution.py:673
  98.2 0.0 copy-start
  98.2 1.4 %copy.13 = f32[3,2048]{1,0:T(4,128)} copy(f32[3,2048]{1,0:T(4,128)} %get-tuple-element.4) | data formatting | bytes 49152
  99.6 0.0 copy-done
  99.6 0.6 copy.14
Async XLA Ops:
  0.6 0.7 copy-start.1
  98.2 1.4 %copy-start = (f32[1,8,768]{2,1,0:T(8,128)S(1)}, f32[1,8,768]{2,1,0:T(8,128)}, u32[]{:S(2)}) copy-start(f32[1,8,768]{2,1,0:T(8,128)} %get-tuple-element.5) | copy-start | bytes 73732

commit v2 on v1

--- a/solution.py
+++ b/solution.py
@@ -18,6 +18,19 @@
 BF16 = jnp.bfloat16
 
 
+UG = 8
+US = 4
+UB = 4
+
+
+def loop(first, last, body, init, unroll):
+    if unroll < last - first:
+        return lax.fori_loop(first, last, body, init, unroll=unroll)
+    for i in range(first, last):
+        init = body(i, init)
+    return init
+
+
 def dot_nn(a, b):
     return lax.dot_general(a, b, (((1,), (0,)), ((), ())), preferred_element_type=F32)
 
@@ -26,22 +39,25 @@
     return lax.dot_general(a, b, (((1,), (1,)), ((), ())), preferred_element_type=F32)
 
 
-def two_pieces(value):
-    high = value.astype(BF16).astype(F32)
-    return high, value - high
+def pieces_of(value, count):
+    found = []
+    for _ in range(count - 1):
+        found.append(value.astype(BF16).astype(F32))
+        value = value - found[-1]
+    return found + [value]
 
 
 def kernel(
     n_blk,
     n_rep,
-    measured_ref,
-    rot_ref,
-    conf_ref,
-    first_ref,
-    second_ref,
-    counts_ref,
-    start_ref,
-    anchor_ref,
+    measured_in,
+    rot_in,
+    conf_in,
+    first_in,
+    second_in,
+    counts_in,
+    start_in,
+    anchor_in,
     est_out,
     weights_out,
     hot,
@@ -91,6 +107,15 @@
     r_g1,
     s_g2,
     r_g2,
+    measured_ref,
+    rot_ref,
+    conf_ref,
+    first_ref,
+    second_ref,
+    counts_ref,
+    start_ref,
+    anchor_ref,
+    s_in,
 ):
     pairs = idx.shape[0] // 3
     tiles = idx.shape[1]
@@ -119,6 +144,22 @@
             device_id_type=MESH,
         )
 
+    pending = []
+
+    def drain():
+        while pending:
+            pending.pop(0)()
+
+    def later(first, last, wait):
+        def loop():
+            def step(k, _):
+                wait(k)
+                return 0
+
+            lax.fori_loop(first, last, step, 0)
+
+        pending.append(loop)
+
     barrier = pltpu.get_barrier_semaphore()
 
     def greet(blk, rep):
@@ -151,19 +192,35 @@
     lax.fori_loop(1, GROUP, greet_inner, 0)
     lax.fori_loop(1, wide, greet_outer, 0)
 
-    def lanes_of(t):
-        return pl.ds(t * LANES, LANES)
-
-    live_all = lax.broadcasted_iota(jnp.int32, first_ref.shape[1:], 1) < counts_ref[0]
-    live_all = jnp.where(live_all, 1.0, 0.0).astype(F32)
+    loads = [
+        pltpu.make_async_copy(src, dst, s_in.at[n])
+        for n, (src, dst) in enumerate(
+            (
+                (start_in, start_ref),
+                (second_in, second_ref),
+                (conf_in, conf_ref),
+                (counts_in, counts_ref),
+                (first_in, first_ref),
+                (rot_in, rot_ref),
+                (measured_in, measured_ref),
+                (anchor_in, anchor_ref),
+            )
+        )
+    ]
+    for load in loads:
+        load.start()
+    for load in loads:
+        load.wait()
+    slot = lax.broadcasted_iota(jnp.int32, (tiles, LANES), 0) * LANES
+    slot = slot + lax.broadcasted_iota(jnp.int32, (tiles, LANES), 1)
     for k in range(pairs):
+        live[k] = jnp.where(slot < counts_ref[0:1, k : k + 1], 1.0, 0.0).astype(F32)
         for t in range(tiles):
             at = slice(t * LANES, (t + 1) * LANES)
-            live[k, t : t + 1] = live_all[k : k + 1, at]
             idx[k, t : t + 1] = first_ref[0, k : k + 1, at]
             idx[2 * pairs + k, t : t + 1] = second_ref[0, k : k + 1, at]
             for c in range(3):
-                conf[k, c, t : t + 1] = conf_ref[c, 0, k : k + 1, at] * live_all[k : k + 1, at]
+                conf[k, c, t : t + 1] = conf_ref[c, 0, k : k + 1, at]
                 meas[k, c, t : t + 1] = measured_ref[c, 0, k : k + 1, at]
                 rotm[k, c, t : t + 1] = rot_ref[c, 0, k : k + 1, at]
     for h in range(HI):
@@ -174,6 +231,7 @@
 
     def stage1(k, _):
         for c in range(3):
+            conf[k, c] = conf[k, c] * live[k]
             send1[k, c] = conf[k, c]
         send1[k, 3] = idx[2 * pairs + k].astype(F32)
         return 0
@@ -198,6 +256,7 @@
         return 0
 
     lax.fori_loop(1, pairs, start_init, 0)
+    later(1, pairs, lambda k: (send_init(k).wait_send(), send_halo(k).wait_send()))
     recv1[0] = send1[0]
 
     def rotations(k, _):
@@ -238,18 +297,22 @@
         build(2 * pairs + k)
         return 0
 
-    def table_of(field):
+    def table_of(field, count):
         rows = []
         for c in range(3):
-            rows.extend(two_pieces(field[c]))
+            rows.extend(pieces_of(field[c], count))
         return jnp.concatenate(rows, axis=0).astype(BF16)
 
     def gather(table, g):
         full = dot_nn(table, hot[g])
         mask = himask[g]
+        count = table.shape[0] // (3 * HI)
         found = []
         for c in range(3):
-            part = (full[16 * c : 16 * c + 8] + full[16 * c + 8 : 16 * c + 16]) * mask
+            part = full[HI * count * c : HI * count * c + HI]
+            for n in range(1, count):
+                part = part + full[HI * (count * c + n) : HI * (count * c + n + 1)]
+            part = part * mask
             row = jnp.sum(part, axis=0, keepdims=True)
             found.append(
                 jnp.concatenate([row[:, t * LANES : (t + 1) * LANES] for t in range(tiles)], axis=0)
@@ -268,11 +331,11 @@
             for i in range(3)
         ]
 
-    lax.fori_loop(0, pairs, build_near, 0)
-    table = table_of(est)
+    loop(0, pairs, build_near, 0, UB)
+    table = table_of(est, 3)
 
     def near_start(i, _):
-        k = lax.rem(i + 1, pairs)
+        k = (i + 1) % pairs
         turned = rotate(k, gather(table, k))
         for c in range(3):
             send2[k, c] = meas[k, c] + turned[c]
@@ -283,10 +346,11 @@
 
         return 0
 
-    lax.fori_loop(0, pairs, near_start, 0)
+    loop(0, pairs, near_start, 0, UG)
+    later(1, pairs, lambda k: send_mis(k).wait_send())
     recv2[0] = send2[0]
 
-    lax.fori_loop(0, pairs, build_second, 0)
+    loop(0, pairs, build_second, 0, UB)
 
     def wait_halo(k, _):
         copy(halo.at[0], halo.at[k], s_init.at[2, k], r_init.at[2, k], b, r).wait_recv()
@@ -295,12 +359,12 @@
     lax.fori_loop(1, pairs, wait_halo, 0)
 
     def own_misfit(k, _):
-        there = gather(table_of(halo.at[k]), 2 * pairs + k)
+        there = gather(table_of(halo.at[k], 3), 2 * pairs + k)
         for c in range(3):
             mis[0, k, c] = send2[k, c] - there[c]
         return 0
 
-    lax.fori_loop(0, pairs, own_misfit, 0)
+    loop(0, pairs, own_misfit, 0, UG)
 
     def wait_init(k, _):
         copy(send1.at[k], recv1.at[k], s_init.at[0, k], r_init.at[0, k], b, r).wait_recv()
@@ -313,7 +377,7 @@
         build(pairs + k)
         return 0
 
-    lax.fori_loop(0, pairs, build_far, 0)
+    loop(0, pairs, build_far, 0, UB)
 
     def wait_mis(k, _):
         copy(send2.at[k], recv2.at[k], s_init.at[1, k], r_init.at[1, k], b, r).wait_recv()
@@ -327,11 +391,11 @@
             mis[1, k, c] = recv2[k, c] - there[c]
         return 0
 
-    lax.fori_loop(0, pairs, far_misfit, 0)
+    loop(0, pairs, far_misfit, 0, UG)
 
     def put(slot, at_row, terms, g):
         for n, term in enumerate(terms):
-            head, tail = two_pieces(term)
+            head, tail = pieces_of(term, 2)
             for t in range(tiles):
                 at = slice(t * LANES, (t + 1) * LANES)
                 mask = himask[g, :, at]
@@ -353,7 +417,7 @@
 
     def exchange_start(x, table):
         def step(i, _):
-            k = lax.rem(i + 1, pairs)
+            k = (i + 1) % pairs
             turned = rotate(k, gather(table, k))
             there = gather(table, pairs + k)
             for c in range(3):
@@ -367,7 +431,8 @@
 
             return 0
 
-        lax.fori_loop(0, pairs, step, 0)
+        loop(0, pairs, step, 0, UG)
+        later(1, pairs, lambda k: (send_back(x, k).wait_send(), send_ahead(x, k).wait_send()))
         xrecv[x, 0, 0] = xsend[x, 0, 0]
         xrecv[x, 1, 0] = xsend[x, 1, 0]
 
@@ -376,6 +441,12 @@
 
     def send_back(x, k):
         return copy(xsend.at[x, 1, k], xrecv.at[x, 1, k], s_x.at[x, 1, k], r_x.at[x, 1, k], behind(k), r)
+
+    def to_twin(src, dst, send, recv, p):
+        both = copy(src.at[p], dst.at[p], send.at[p], recv.at[p], b, 1 - r)
+        both.start()
+        pending.append(both.wait_send)
+        both.wait_recv()
 
     def wait_exchange(x, k):
         @pl.when(k != 0)
@@ -385,7 +456,7 @@
 
     lane = lax.broadcasted_iota(jnp.int32, (1, LANES), 1)
 
-    for p in range(PASSES):
+    def one_pass(p, _):
         def near_sums(k, totals):
             m = [mis[0, k, c] for c in range(3)]
             cf = [conf[k, c] for c in range(3)]
@@ -404,8 +475,8 @@
                     + rot[1][f] * wc[1] * rot[1][s]
                     + rot[2][f] * wc[2] * rot[2][s]
                 )
-            put(0, 0, terms, k)
-            return totals + dot_nt(lhs[0], hot[k])
+            put(k, 0, terms, k)
+            return totals + dot_nt(lhs[k], hot[k])
 
         def far_sums(k, totals):
             m = [mis[1, k, c] for c in range(3)]
@@ -415,19 +486,18 @@
             wc = [weight * cf[c] for c in range(3)]
             for c in range(3):
                 wconf[1, k, c] = wc[c]
-            put(1, 0, [wc[c] * m[c] for c in range(3)] + wc, pairs + k)
-            return totals + dot_nt(lhs[1, 0:96], hot[pairs + k])
-
-        near = lax.fori_loop(0, pairs, near_sums, jnp.zeros((144, lo_count), F32))
-        far = lax.fori_loop(0, pairs, far_sums, jnp.zeros((96, lo_count), F32))
+            put(pairs + k, 0, [wc[c] * m[c] for c in range(3)] + wc, pairs + k)
+            return totals + dot_nt(lhs[pairs + k, 0:96], hot[pairs + k])
+
+        near = loop(0, pairs, near_sums, jnp.zeros((144, lo_count), F32), US)
+        far = loop(0, pairs, far_sums, jnp.zeros((96, lo_count), F32), US)
         for n in range(9):
             total = summed(near, n)
             spot = {0: 0, 1: 1, 2: 2, 3: 3, 6: 4, 8: 5}.get(n)
             if spot is not None:
                 total = total + summed(far, spot)
             bsend[p, n] = total
-        copy(bsend.at[p], brecv.at[p], s_b.at[p], r_b.at[p], b, 1 - r).start()
-        copy(bsend.at[p], brecv.at[p], s_b.at[p], r_b.at[p], b, 1 - r).wait_recv()
+        to_twin(bsend, brecv, s_b, r_b, p)
         anchor = anc[...]
         for c in range(3):
             fr[c] = bsend[p, c] + brecv[p, c] - anchor * est[c]
@@ -449,7 +519,7 @@
         invert(fr, fz)
 
         x = 2 * p
-        exchange_start(x, table_of(fz))
+        exchange_start(x, table_of(fz, 2))
 
         def product_near(k, totals):
             wait_exchange(x, k)
@@ -460,8 +530,8 @@
                 chz[0, k, c] = change[c]
                 pushed.append(wconf[0, k, c] * change[c])
                 square = square + pushed[c] * change[c]
-            put(0, 0, [-value for value in rotate_back(k, pushed)], k)
-            return totals[0] + dot_nt(lhs[0, 0:48], hot[k]), square
+            put(k, 0, [-value for value in rotate_back(k, pushed)], k)
+            return totals[0] + dot_nt(lhs[k, 0:48], hot[k]), square
 
         def product_far(k, totals):
             change = [xsend[x, 1, k, c] - xrecv[x, 0, k, c] for c in range(3)]
@@ -469,24 +539,23 @@
             for c in range(3):
                 chz[1, k, c] = change[c]
                 pushed.append(wconf[1, k, c] * change[c])
-            put(1, 0, pushed, pairs + k)
-            return totals + dot_nt(lhs[1, 0:48], hot[pairs + k])
+            put(pairs + k, 0, pushed, pairs + k)
+            return totals + dot_nt(lhs[pairs + k, 0:48], hot[pairs + k])
 
         zero_row = jnp.zeros((tiles, LANES), F32)
-        totals, z_square = lax.fori_loop(
-            0, pairs, product_near, (jnp.zeros((48, lo_count), F32), zero_row)
+        totals, z_square = loop(
+            0, pairs, product_near, (jnp.zeros((48, lo_count), F32), zero_row), US
         )
-        totals = lax.fori_loop(0, pairs, product_far, totals)
+        totals = loop(0, pairs, product_far, totals, US)
         for c in range(3):
             dsend[p, c] = summed(totals, c)
-        copy(dsend.at[p], drecv.at[p], s_d.at[p], r_d.at[p], b, 1 - r).start()
-        copy(dsend.at[p], drecv.at[p], s_d.at[p], r_d.at[p], b, 1 - r).wait_recv()
+        to_twin(dsend, drecv, s_d, r_d, p)
         for c in range(3):
             fq[c] = dsend[p, c] + drecv[p, c] + anchor * fz[c]
         invert(fq, fu)
 
         y = 2 * p + 1
-        exchange_start(y, table_of(fu))
+        exchange_start(y, table_of(fu, 2))
 
         def change_u(k, square):
             wait_exchange(y, k)
@@ -523,6 +592,14 @@
                 return 0
 
             lax.fori_loop(1, count, start, 0)
+            drain()
+            later(
+                1,
+                count,
+                lambda j: copy(
+                    send_ref.at[p], recv_ref.at[p, me], s_sem.at[p, j], r_sem.at[p, me], b, r
+                ).wait_send(),
+            )
             recv_ref[p, me] = row
 
             def wait(j, _):
@@ -555,8 +632,8 @@
         of_u = -alpha * alpha_two
         for c in range(3):
             est[c] = est[c] + of_z * fz[c] + of_u * fu[c]
-        if p + 1 < PASSES:
-
+        @pl.when(p + 1 < PASSES)
+        def _():
             def new_misfit(k, _):
                 for side in range(2):
                     for c in range(3):
@@ -567,6 +644,12 @@
 
             lax.fori_loop(0, pairs, new_misfit, 0)
 
+        drain()
+        return 0
+
+    drain()
+    lax.fori_loop(0, PASSES, one_pass, 0)
+
     for k in range(pairs):
         for t in range(tiles):
             weights_out[0, k : k + 1, t * LANES : (t + 1) * LANES] = wout[k, t : t + 1]
@@ -574,24 +657,6 @@
         at = slice(h * lo_count, (h + 1) * lo_count)
         for c in range(3):
             est_out[c : c + 1, at] = est[c, h : h + 1]
-
-    def drain_init(k, _):
-        send_init(k).wait_send()
-        send_mis(k).wait_send()
-        send_halo(k).wait_send()
-        for x in range(2 * PASSES):
-            send_ahead(x, k).wait_send()
-            send_back(x, k).wait_send()
-        return 0
-
-    lax.fori_loop(1, pairs, drain_init, 0)
-    for p in range(PASSES):
-        copy(bsend.at[p], brecv.at[p], s_b.at[p], r_b.at[p], b, 1 - r).wait_send()
-        copy(dsend.at[p], drecv.at[p], s_d.at[p], r_d.at[p], b, 1 - r).wait_send()
-        for j in range(1, GROUP):
-            copy(g1send.at[p], g1recv.at[p, 0], s_g1.at[p, j], r_g1.at[p, 0], b, r).wait_send()
-        for j in range(1, wide):
-            copy(g2send.at[p], g2recv.at[p, 0], s_g2.at[p, j], r_g2.at[p, 0], b, r).wait_send()
 
 
 def on_device(
@@ -655,7 +720,7 @@
         vmem((PASSES, GROUP, 1, LANES), F32),
         vmem((PASSES, 1, LANES), F32),
         vmem((PASSES, wide, 1, LANES), F32),
-        vmem((2, 144, slots), BF16),
+        vmem((2 * pairs, 144, slots), BF16),
         sem((3, pairs)),
         sem((3, pairs)),
         sem((PASSES,)),
@@ -668,15 +733,24 @@
         sem((PASSES, GROUP)),
         sem((PASSES, wide)),
         sem((PASSES, wide)),
+        vmem(measured.shape, F32),
+        vmem(rot_vector.shape, F32),
+        vmem(confidence.shape, F32),
+        vmem(first_local.shape, jnp.int32),
+        vmem(second_local.shape, jnp.int32),
+        vmem((1, pairs), jnp.int32),
+        vmem(start_angles.shape, F32),
+        vmem((1, cams), F32),
+        sem((8,)),
     ]
     whole = pl.BlockSpec(memory_space=pltpu.VMEM)
     return pl.pallas_call(
         functools.partial(kernel, n_blk, n_rep),
         out_shape=(
-            jax.ShapeDtypeStruct((3, cams), F32),
-            jax.ShapeDtypeStruct((1, pairs, slots), F32),
+            pltpu.VMEM((3, cams), F32),
+            pltpu.VMEM((1, pairs, slots), F32),
         ),
-        in_specs=[whole] * 8,
+        in_specs=[pl.BlockSpec(memory_space=pl.ANY)] * 8,
         out_specs=(whole, whole),
         scratch_shapes=scratch,
         compiler_params=pltpu.CompilerParams(
@@ -688,7 +762,7 @@
         confidence,
         first_local,
         second_local,
-        edge_counts,
+        edge_counts.reshape(1, -1),
         start_angles,
         anchor.reshape(1, -1),
     )

time: 101 us -> 88.9 us (0.88)
  Pallas kernels: 96.3 us -> 86.7 us
  local copies, waits for them, and re-layouts: 3.32 us -> 1.22 us
    pallas_call x1, Pallas kernels: 96.3 us -> 86.7 us  [on_device(): pl.pallas_call(functools.partial(kernel, n_blk, n_rep), out_shape=(pltpu....]
    unnamed x7 -> x2, local copies, waits for them, and re-layouts: 3.32 us -> 1.22 us
where the time goes in v2:
time: 88.9 us; the launch traced here: 88.6 us
  Pallas kernels  86.7 us (98%)
  local copies, waits for them, and re-layouts  1.22 us (1%)
    pallas_call x1, Pallas kernels, on_device(): pl.pallas_call(functools.partial(kernel, n_blk, n_rep), out_shape=(pltpu....  86.7 us

profile of v2, /device:TPU:1, one launch (start us, length us, event | category | flops | bytes accessed | tf_op | source)
XLA Modules:
  0.0 88.6 jit_solution(1109021789297570495)
XLA Ops:
  0.6 86.7 %shard_map.95 = (f32[3,2048]{1,0:T(4,128)S(1)}, f32[1,8,768]{2,1,0:T(8,128)S(1)}) custom-call(f32[3,1,8,768]{3,2,1,0:T(8,128)} %measured_in.1, f32[3,1,8,768]{3,2,1,0:T(8,128)} %rot_in.1, f32[3,1,8,768]{3,2,1,0:T(8,128)} %conf_in.1, s32[1,8,768]{2,1,0:T(8,128)} %first_in.1, s32[1,8,768]{2,1,0:T(8,128)} %second_in.1, s32[1,8]{1,0:T(1,128)} %bitcast.3, ...), custom_call_target="tpu_custom_call" | custom-call | tf_op jit(solution)/shard_map/pallas_call | solution.py:747
  87.4 0.6 copy.12
  88.0 0.6 copy.13

commit v3 on v2

--- a/solution.py
+++ b/solution.py
@@ -11,9 +11,10 @@
 SOFTEN = 0.05
 MESH = pl.DeviceIdType.MESH
 LANES = 128
-HI = 8
+HI = 16
 GROUP = 8
-PAIRS = ((0, 0), (0, 1), (0, 2), (1, 1), (1, 2), (2, 2))
+DIAGONAL = ((0, 0), (1, 1), (2, 2))
+OTHERS = ((0, 1), (0, 2), (1, 2))
 F32 = jnp.float32
 BF16 = jnp.bfloat16
 
@@ -119,6 +120,7 @@
 ):
     pairs = idx.shape[0] // 3
     tiles = idx.shape[1]
+    rows_of = 2 * HI
     lo_count = est.shape[2]
     outer = n_blk // GROUP
     wide = outer * n_rep
@@ -165,12 +167,11 @@
     def greet(blk, rep):
         pl.semaphore_signal(barrier, inc=1, device_id={"blk": blk, "rep": rep}, device_id_type=MESH)
 
-    def greet_pairs(k, _):
-        greet(ahead(k), r)
-        greet(behind(k), r)
-        return 0
-
-    lax.fori_loop(1, pairs, greet_pairs, 0)
+    ahead_of = [ahead(k) for k in range(pairs)]
+    behind_of = [behind(k) for k in range(pairs)]
+    for k in range(1, pairs):
+        greet(ahead_of[k], r)
+        greet(behind_of[k], r)
     greet(b, 1 - r)
 
     def inner_peer(j):
@@ -180,17 +181,10 @@
         other = lax.rem(mine2 + j, wide)
         return (other // n_rep) * GROUP + low, lax.rem(other, n_rep)
 
-    def greet_inner(j, _):
-        greet(inner_peer(j), r)
-        return 0
-
-    def greet_outer(j, _):
-        blk, rep = outer_peer(j)
+    inner_of = [(inner_peer(j), r) for j in range(GROUP)]
+    outer_of = [outer_peer(j) for j in range(wide)]
+    for blk, rep in inner_of[1:] + outer_of[1:]:
         greet(blk, rep)
-        return 0
-
-    lax.fori_loop(1, GROUP, greet_inner, 0)
-    lax.fori_loop(1, wide, greet_outer, 0)
 
     loads = [
         pltpu.make_async_copy(src, dst, s_in.at[n])
@@ -239,25 +233,19 @@
     lax.fori_loop(0, pairs, stage1, 0)
     halo[0] = est[...]
 
+    def send_init(k, blk):
+        return copy(send1.at[k], recv1.at[k], s_init.at[0, k], r_init.at[0, k], blk, r)
+
+    def send_mis(k, blk):
+        return copy(send2.at[k], recv2.at[k], s_init.at[1, k], r_init.at[1, k], blk, r)
+
+    def send_halo(k, blk):
+        return copy(halo.at[0], halo.at[k], s_init.at[2, k], r_init.at[2, k], blk, r)
+
     pl.semaphore_wait(barrier, 2 * (pairs - 1) + 1 + (GROUP - 1) + (wide - 1))
-
-    def send_init(k):
-        return copy(send1.at[k], recv1.at[k], s_init.at[0, k], r_init.at[0, k], ahead(k), r)
-
-    def send_mis(k):
-        return copy(send2.at[k], recv2.at[k], s_init.at[1, k], r_init.at[1, k], ahead(k), r)
-
-    def send_halo(k):
-        return copy(halo.at[0], halo.at[k], s_init.at[2, k], r_init.at[2, k], behind(k), r)
-
-    def start_init(k, _):
-        send_init(k).start()
-        send_halo(k).start()
-        return 0
-
-    lax.fori_loop(1, pairs, start_init, 0)
-    later(1, pairs, lambda k: (send_init(k).wait_send(), send_halo(k).wait_send()))
-    recv1[0] = send1[0]
+    for k in range(1, pairs):
+        send_halo(k, behind_of[k]).start()
+        send_init(k, ahead_of[k]).start()
 
     def rotations(k, _):
         v = [rotm[k, c] for c in range(3)]
@@ -334,43 +322,26 @@
     loop(0, pairs, build_near, 0, UB)
     table = table_of(est, 3)
 
-    def near_start(i, _):
-        k = (i + 1) % pairs
+    def near_start(k, _):
         turned = rotate(k, gather(table, k))
         for c in range(3):
             send2[k, c] = meas[k, c] + turned[c]
-
-        @pl.when(k != 0)
-        def _():
-            send_mis(k).start()
-
-        return 0
-
-    loop(0, pairs, near_start, 0, UG)
-    later(1, pairs, lambda k: send_mis(k).wait_send())
+        if k != 0:
+            send_mis(k, ahead_of[k]).start()
+        return 0
+
+    loop(0, pairs, near_start, 0, pairs)
+    loop(0, pairs, build_second, 0, UB)
+    later(
+        1,
+        pairs,
+        lambda k: [send(k, b).wait_send() for send in (send_init, send_mis, send_halo)],
+    )
+    recv1[0] = send1[0]
     recv2[0] = send2[0]
 
-    loop(0, pairs, build_second, 0, UB)
-
-    def wait_halo(k, _):
-        copy(halo.at[0], halo.at[k], s_init.at[2, k], r_init.at[2, k], b, r).wait_recv()
-        return 0
-
-    lax.fori_loop(1, pairs, wait_halo, 0)
-
-    def own_misfit(k, _):
-        there = gather(table_of(halo.at[k], 3), 2 * pairs + k)
-        for c in range(3):
-            mis[0, k, c] = send2[k, c] - there[c]
-        return 0
-
-    loop(0, pairs, own_misfit, 0, UG)
-
-    def wait_init(k, _):
-        copy(send1.at[k], recv1.at[k], s_init.at[0, k], r_init.at[0, k], b, r).wait_recv()
-        return 0
-
-    lax.fori_loop(1, pairs, wait_init, 0)
+    for k in range(1, pairs):
+        send_init(k, b).wait_recv()
 
     def build_far(k, _):
         idx[pairs + k] = recv1[k, 3].astype(jnp.int32)
@@ -379,19 +350,25 @@
 
     loop(0, pairs, build_far, 0, UB)
 
-    def wait_mis(k, _):
-        copy(send2.at[k], recv2.at[k], s_init.at[1, k], r_init.at[1, k], b, r).wait_recv()
-        return 0
-
-    lax.fori_loop(1, pairs, wait_mis, 0)
-
     def far_misfit(k, _):
         there = gather(table, pairs + k)
         for c in range(3):
             mis[1, k, c] = recv2[k, c] - there[c]
         return 0
 
+    for k in range(1, pairs):
+        send_mis(k, b).wait_recv()
     loop(0, pairs, far_misfit, 0, UG)
+    for k in range(1, pairs):
+        send_halo(k, b).wait_recv()
+
+    def own_misfit(k, _):
+        there = gather(table_of(halo.at[k], 3), 2 * pairs + k)
+        for c in range(3):
+            mis[0, k, c] = send2[k, c] - there[c]
+        return 0
+
+    loop(0, pairs, own_misfit, 0, UG)
 
     def put(slot, at_row, terms, g):
         for n, term in enumerate(terms):
@@ -400,10 +377,11 @@
                 at = slice(t * LANES, (t + 1) * LANES)
                 mask = himask[g, :, at]
                 both = jnp.concatenate([head[t : t + 1] * mask, tail[t : t + 1] * mask], axis=0)
-                lhs[slot, at_row + 16 * n : at_row + 16 * n + 16, at] = both.astype(BF16)
+                lhs[slot, at_row + rows_of * n : at_row + rows_of * (n + 1), at] = both.astype(BF16)
 
     def summed(totals, channel):
-        return totals[16 * channel : 16 * channel + 8] + totals[16 * channel + 8 : 16 * channel + 16]
+        at = rows_of * channel
+        return totals[at : at + HI] + totals[at + HI : at + rows_of]
 
     def full_sum(value):
         return jnp.sum(jnp.sum(value, axis=0, keepdims=True), axis=1, keepdims=True)
@@ -424,35 +402,36 @@
                 xsend[x, 0, k, c] = turned[c]
                 xsend[x, 1, k, c] = there[c]
 
-            @pl.when(k != 0)
-            def _():
-                send_back(x, k).start()
-                send_ahead(x, k).start()
+            if k != 0:
+                send_back(x, k, behind_of[k]).start()
+                send_ahead(x, k, ahead_of[k]).start()
 
             return 0
 
-        loop(0, pairs, step, 0, UG)
-        later(1, pairs, lambda k: (send_back(x, k).wait_send(), send_ahead(x, k).wait_send()))
+        loop(0, pairs, step, 0, pairs)
+        later(1, pairs, lambda k: (send_back(x, k, b).wait_send(), send_ahead(x, k, b).wait_send()))
         xrecv[x, 0, 0] = xsend[x, 0, 0]
         xrecv[x, 1, 0] = xsend[x, 1, 0]
 
-    def send_ahead(x, k):
-        return copy(xsend.at[x, 0, k], xrecv.at[x, 0, k], s_x.at[x, 0, k], r_x.at[x, 0, k], ahead(k), r)
-
-    def send_back(x, k):
-        return copy(xsend.at[x, 1, k], xrecv.at[x, 1, k], s_x.at[x, 1, k], r_x.at[x, 1, k], behind(k), r)
-
-    def to_twin(src, dst, send, recv, p):
-        both = copy(src.at[p], dst.at[p], send.at[p], recv.at[p], b, 1 - r)
+    def send_ahead(x, k, blk):
+        return copy(xsend.at[x, 0, k], xrecv.at[x, 0, k], s_x.at[x, 0, k], r_x.at[x, 0, k], blk, r)
+
+    def send_back(x, k, blk):
+        return copy(xsend.at[x, 1, k], xrecv.at[x, 1, k], s_x.at[x, 1, k], r_x.at[x, 1, k], blk, r)
+
+    def to_twin(src, dst, send, recv):
+        both = copy(src, dst, send, recv, b, 1 - r)
         both.start()
         pending.append(both.wait_send)
-        both.wait_recv()
-
-    def wait_exchange(x, k):
-        @pl.when(k != 0)
-        def _():
-            copy(xsend.at[x, 1, k], xrecv.at[x, 1, k], s_x.at[x, 1, k], r_x.at[x, 1, k], b, r).wait_recv()
-            copy(xsend.at[x, 0, k], xrecv.at[x, 0, k], s_x.at[x, 0, k], r_x.at[x, 0, k], b, r).wait_recv()
+        return both.wait_recv
+
+    def wait_back(x, k):
+        if k != 0:
+            send_back(x, k, b).wait_recv()
+
+    def wait_ahead(x, k):
+        if k != 0:
+            send_ahead(x, k, b).wait_recv()
 
     lane = lax.broadcasted_iota(jnp.int32, (1, LANES), 1)
 
@@ -469,7 +448,7 @@
             back = rotate_back(k, [wc[c] * m[c] for c in range(3)])
             rot = [[rotm[k, 3 * i + j] for j in range(3)] for i in range(3)]
             terms = [-value for value in back]
-            for f, s in PAIRS:
+            for f, s in DIAGONAL + OTHERS:
                 terms.append(
                     rot[0][f] * wc[0] * rot[0][s]
                     + rot[1][f] * wc[1] * rot[1][s]
@@ -487,24 +466,24 @@
             for c in range(3):
                 wconf[1, k, c] = wc[c]
             put(pairs + k, 0, [wc[c] * m[c] for c in range(3)] + wc, pairs + k)
-            return totals + dot_nt(lhs[pairs + k, 0:96], hot[pairs + k])
-
-        near = loop(0, pairs, near_sums, jnp.zeros((144, lo_count), F32), US)
-        far = loop(0, pairs, far_sums, jnp.zeros((96, lo_count), F32), US)
-        for n in range(9):
-            total = summed(near, n)
-            spot = {0: 0, 1: 1, 2: 2, 3: 3, 6: 4, 8: 5}.get(n)
-            if spot is not None:
-                total = total + summed(far, spot)
-            bsend[p, n] = total
-        to_twin(bsend, brecv, s_b, r_b, p)
+            return totals + dot_nt(lhs[pairs + k, 0 : 6 * rows_of], hot[pairs + k])
+
+        near = loop(0, pairs, near_sums, jnp.zeros((9 * rows_of, lo_count), F32), US)
+        for n in range(6, 9):
+            bsend[p, n] = summed(near, n)
+        finish_others = to_twin(bsend.at[p, 6:9], brecv.at[p, 6:9], s_b.at[p, 1], r_b.at[p, 1])
+        far = loop(0, pairs, far_sums, jnp.zeros((6 * rows_of, lo_count), F32), US)
+        for n in range(6):
+            bsend[p, n] = summed(near, n) + summed(far, n)
+        finish_first = to_twin(bsend.at[p, 0:6], brecv.at[p, 0:6], s_b.at[p, 0], r_b.at[p, 0])
+        finish_others()
+        finish_first()
         anchor = anc[...]
         for c in range(3):
             fr[c] = bsend[p, c] + brecv[p, c] - anchor * est[c]
-        blocks = []
-        for n, (f, s) in enumerate(PAIRS):
-            block = bsend[p, 3 + n] + brecv[p, 3 + n]
-            blocks.append(block + anchor if f == s else block)
+        diagonal = [bsend[p, 3 + n] + brecv[p, 3 + n] + anchor for n in range(3)]
+        others = [bsend[p, 6 + n] + brecv[p, 6 + n] for n in range(3)]
+        blocks = [diagonal[0], others[0], others[1], diagonal[1], others[2], diagonal[2]]
         adjugate = [
             blocks[3] * blocks[5] - blocks[4] * blocks[4],
             blocks[2] * blocks[4] - blocks[1] * blocks[5],
@@ -522,7 +501,7 @@
         exchange_start(x, table_of(fz, 2))
 
         def product_near(k, totals):
-            wait_exchange(x, k)
+            wait_back(x, k)
             change = [xrecv[x, 1, k, c] - xsend[x, 0, k, c] for c in range(3)]
             pushed = []
             square = totals[1]
@@ -531,25 +510,26 @@
                 pushed.append(wconf[0, k, c] * change[c])
                 square = square + pushed[c] * change[c]
             put(k, 0, [-value for value in rotate_back(k, pushed)], k)
-            return totals[0] + dot_nt(lhs[k, 0:48], hot[k]), square
+            return totals[0] + dot_nt(lhs[k, 0 : 3 * rows_of], hot[k]), square
 
         def product_far(k, totals):
+            wait_ahead(x, k)
             change = [xsend[x, 1, k, c] - xrecv[x, 0, k, c] for c in range(3)]
             pushed = []
             for c in range(3):
                 chz[1, k, c] = change[c]
                 pushed.append(wconf[1, k, c] * change[c])
             put(pairs + k, 0, pushed, pairs + k)
-            return totals + dot_nt(lhs[pairs + k, 0:48], hot[pairs + k])
+            return totals + dot_nt(lhs[pairs + k, 0 : 3 * rows_of], hot[pairs + k])
 
         zero_row = jnp.zeros((tiles, LANES), F32)
         totals, z_square = loop(
-            0, pairs, product_near, (jnp.zeros((48, lo_count), F32), zero_row), US
+            0, pairs, product_near, (jnp.zeros((3 * rows_of, lo_count), F32), zero_row), pairs
         )
-        totals = loop(0, pairs, product_far, totals, US)
+        totals = loop(0, pairs, product_far, totals, pairs)
         for c in range(3):
             dsend[p, c] = summed(totals, c)
-        to_twin(dsend, drecv, s_d, r_d, p)
+        to_twin(dsend.at[p], drecv.at[p], s_d.at[p], r_d.at[p])()
         for c in range(3):
             fq[c] = dsend[p, c] + drecv[p, c] + anchor * fz[c]
         invert(fq, fu)
@@ -558,15 +538,14 @@
         exchange_start(y, table_of(fu, 2))
 
         def change_u(k, square):
-            wait_exchange(y, k)
+            wait_back(y, k)
             for c in range(3):
                 change = xrecv[y, 1, k, c] - xsend[y, 0, k, c]
-                chu[0, k, c] = change
+                chu[k, c] = change
                 square = square + wconf[0, k, c] * change * change
-                chu[1, k, c] = xsend[y, 1, k, c] - xrecv[y, 0, k, c]
             return square
 
-        u_square = lax.fori_loop(0, pairs, change_u, zero_row)
+        u_square = loop(0, pairs, change_u, zero_row, pairs)
 
         half = 1.0 / n_rep
         rz = fr[0] * fz[0] + fr[1] * fz[1] + fr[2] * fz[2]
@@ -583,40 +562,35 @@
         for n, part in enumerate(parts):
             row = jnp.where(lane == n, part, row)
 
-        def reduce_over(row, send_ref, recv_ref, s_sem, r_sem, count, me, peer):
+        def reduce_over(row, send_ref, recv_ref, s_sem, r_sem, me, peers, meanwhile):
+            count = len(peers)
             send_ref[p] = row
 
-            def start(j, _):
-                blk, rep = peer(j)
-                copy(send_ref.at[p], recv_ref.at[p, me], s_sem.at[p, j], r_sem.at[p, me], blk, rep).start()
-                return 0
-
-            lax.fori_loop(1, count, start, 0)
-            drain()
-            later(
-                1,
-                count,
-                lambda j: copy(
-                    send_ref.at[p], recv_ref.at[p, me], s_sem.at[p, j], r_sem.at[p, me], b, r
-                ).wait_send(),
-            )
+            def send(j, at, blk, rep):
+                return copy(
+                    send_ref.at[p], recv_ref.at[p, at], s_sem.at[p, j], r_sem.at[p, at], blk, rep
+                )
+
+            for j in range(1, count):
+                send(j, me, *peers[j]).start()
+            meanwhile()
+            later(1, count, lambda j: send(j, me, b, r).wait_send())
             recv_ref[p, me] = row
-
-            def wait(j, _):
-                other = lax.rem(me + j, count)
-                copy(send_ref.at[p], recv_ref.at[p, other], s_sem.at[p, j], r_sem.at[p, other], b, r).wait_recv()
-                return 0
-
-            lax.fori_loop(1, count, wait, 0)
+            for j in range(1, count):
+                send(j, lax.rem(me + j, count), b, r).wait_recv()
             total = recv_ref[p, 0]
             for n in range(1, count):
                 total = total + recv_ref[p, n]
             return total
 
-        row = reduce_over(
-            row, g1send, g1recv, s_g1, r_g1, GROUP, low, lambda j: (inner_peer(j), r)
-        )
-        row = reduce_over(row, g2send, g2recv, s_g2, r_g2, wide, mine2, outer_peer)
+        def write_weights():
+            drain()
+            for k in range(pairs):
+                for t in range(tiles):
+                    weights_out[0, k : k + 1, t * LANES : (t + 1) * LANES] = wout[k, t : t + 1]
+
+        row = reduce_over(row, g1send, g1recv, s_g1, r_g1, low, inner_of, drain)
+        row = reduce_over(row, g2send, g2recv, s_g2, r_g2, mine2, outer_of, write_weights)
 
         def scalar(n):
             return jnp.sum(jnp.where(lane == n, row, 0.0), axis=1, keepdims=True)
@@ -632,27 +606,21 @@
         of_u = -alpha * alpha_two
         for c in range(3):
             est[c] = est[c] + of_z * fz[c] + of_u * fu[c]
-        @pl.when(p + 1 < PASSES)
-        def _():
-            def new_misfit(k, _):
-                for side in range(2):
-                    for c in range(3):
-                        mis[side, k, c] = (
-                            mis[side, k, c] - of_z * chz[side, k, c] - of_u * chu[side, k, c]
-                        )
-                return 0
-
-            lax.fori_loop(0, pairs, new_misfit, 0)
-
+        def new_misfit(k, _):
+            wait_ahead(y, k)
+            for c in range(3):
+                mis[0, k, c] = mis[0, k, c] - of_z * chz[0, k, c] - of_u * chu[k, c]
+                far_u = xsend[y, 1, k, c] - xrecv[y, 0, k, c]
+                mis[1, k, c] = mis[1, k, c] - of_z * chz[1, k, c] - of_u * far_u
+            return 0
+
+        loop(0, pairs, new_misfit, 0, pairs)
         drain()
         return 0
 
     drain()
     lax.fori_loop(0, PASSES, one_pass, 0)
 
-    for k in range(pairs):
-        for t in range(tiles):
-            weights_out[0, k : k + 1, t * LANES : (t + 1) * LANES] = wout[k, t : t + 1]
     for h in range(HI):
         at = slice(h * lo_count, (h + 1) * lo_count)
         for c in range(3):
@@ -697,7 +665,7 @@
         edges(2, pairs, 3),
         edges(2, pairs, 3),
         edges(2, pairs, 3),
-        edges(2, pairs, 3),
+        edges(pairs, 3),
         edges(pairs, 4),
         edges(pairs, 4),
         edges(pairs, 3),
@@ -720,11 +688,11 @@
         vmem((PASSES, GROUP, 1, LANES), F32),
         vmem((PASSES, 1, LANES), F32),
         vmem((PASSES, wide, 1, LANES), F32),
-        vmem((2 * pairs, 144, slots), BF16),
+        vmem((2 * pairs, 18 * HI, slots), BF16),
         sem((3, pairs)),
         sem((3, pairs)),
-        sem((PASSES,)),
-        sem((PASSES,)),
+        sem((PASSES, 2)),
+        sem((PASSES, 2)),
         sem((PASSES,)),
         sem((PASSES,)),
         sem((2 * PASSES, 2, pairs)),

time: 88.9 us -> 84.4 us (0.949)
  Pallas kernels: 86.7 us -> 82.2 us
    pallas_call x1, Pallas kernels: 86.7 us -> 82.2 us  [on_device(): pl.pallas_call(functools.partial(kernel, n_blk, n_rep), out_shape=(pltpu....]
where the time goes in v3:
time: 84.4 us; the launch traced here: 84.1 us
  Pallas kernels  82.2 us (97%)
  local copies, waits for them, and re-layouts  1.22 us (1%)
    pallas_call x1, Pallas kernels, on_device(): pl.pallas_call(functools.partial(kernel, n_blk, n_rep), out_shape=(pltpu....  82.2 us

profile of v3, /device:TPU:1, one launch (start us, length us, event | category | flops | bytes accessed | tf_op | source)
XLA Modules:
  0.0 84.1 jit_solution(14430365792507404849)
XLA Ops:
  0.6 82.2 %shard_map.95 = (f32[3,2048]{1,0:T(4,128)S(1)}, f32[1,8,768]{2,1,0:T(8,128)S(1)}) custom-call(f32[3,1,8,768]{3,2,1,0:T(8,128)} %measured_in.1, f32[3,1,8,768]{3,2,1,0:T(8,128)} %rot_in.1, f32[3,1,8,768]{3,2,1,0:T(8,128)} %conf_in.1, s32[1,8,768]{2,1,0:T(8,128)} %first_in.1, s32[1,8,768]{2,1,0:T(8,128)} %second_in.1, s32[1,8]{1,0:T(1,128)} %bitcast.3, ...), custom_call_target="tpu_custom_call" | custom-call | tf_op jit(solution)/shard_map/pallas_call | solution.py:715
  82.8 0.6 copy.12
  83.4 0.6 copy.13

commit v4 on v3

--- a/solution.py
+++ b/solution.py
@@ -12,7 +12,6 @@
 MESH = pl.DeviceIdType.MESH
 LANES = 128
 HI = 16
-GROUP = 8
 DIAGONAL = ((0, 0), (1, 1), (2, 2))
 OTHERS = ((0, 1), (0, 2), (1, 2))
 F32 = jnp.float32
@@ -22,6 +21,7 @@
 UG = 8
 US = 4
 UB = 4
+UJ = 8
 
 
 def loop(first, last, body, init, unroll):
@@ -91,10 +91,8 @@
     drecv,
     xsend,
     xrecv,
-    g1send,
-    g1recv,
-    g2send,
-    g2recv,
+    gsend,
+    grecv,
     lhs,
     s_init,
     r_init,
@@ -104,10 +102,8 @@
     r_d,
     s_x,
     r_x,
-    s_g1,
-    r_g1,
-    s_g2,
-    r_g2,
+    s_g,
+    r_g,
     measured_ref,
     rot_ref,
     conf_ref,
@@ -122,13 +118,8 @@
     tiles = idx.shape[1]
     rows_of = 2 * HI
     lo_count = est.shape[2]
-    outer = n_blk // GROUP
-    wide = outer * n_rep
     b = lax.axis_index("blk")
     r = lax.axis_index("rep")
-    low = lax.rem(b, GROUP)
-    high = b // GROUP
-    mine2 = high * n_rep + r
 
     def ahead(k):
         return lax.rem(b + k, n_blk)
@@ -161,30 +152,6 @@
             lax.fori_loop(first, last, step, 0)
 
         pending.append(loop)
-
-    barrier = pltpu.get_barrier_semaphore()
-
-    def greet(blk, rep):
-        pl.semaphore_signal(barrier, inc=1, device_id={"blk": blk, "rep": rep}, device_id_type=MESH)
-
-    ahead_of = [ahead(k) for k in range(pairs)]
-    behind_of = [behind(k) for k in range(pairs)]
-    for k in range(1, pairs):
-        greet(ahead_of[k], r)
-        greet(behind_of[k], r)
-    greet(b, 1 - r)
-
-    def inner_peer(j):
-        return high * GROUP + lax.rem(low + j, GROUP)
-
-    def outer_peer(j):
-        other = lax.rem(mine2 + j, wide)
-        return (other // n_rep) * GROUP + low, lax.rem(other, n_rep)
-
-    inner_of = [(inner_peer(j), r) for j in range(GROUP)]
-    outer_of = [outer_peer(j) for j in range(wide)]
-    for blk, rep in inner_of[1:] + outer_of[1:]:
-        greet(blk, rep)
 
     loads = [
         pltpu.make_async_copy(src, dst, s_in.at[n])
@@ -203,6 +170,22 @@
     ]
     for load in loads:
         load.start()
+
+    barrier = pltpu.get_barrier_semaphore()
+
+    ahead_of = [ahead(k) for k in range(pairs)]
+    behind_of = [behind(k) for k in range(pairs)]
+    count = n_blk * n_rep
+    me = b * n_rep + r
+
+    def greet(j, _):
+        pl.semaphore_signal(
+            barrier, inc=1, device_id=lax.rem(me + j, count), device_id_type=pl.DeviceIdType.LOGICAL
+        )
+        return 0
+
+    lax.fori_loop(1, count, greet, 0, unroll=UJ)
+
     for load in loads:
         load.wait()
     slot = lax.broadcasted_iota(jnp.int32, (tiles, LANES), 0) * LANES
@@ -242,7 +225,7 @@
     def send_halo(k, blk):
         return copy(halo.at[0], halo.at[k], s_init.at[2, k], r_init.at[2, k], blk, r)
 
-    pl.semaphore_wait(barrier, 2 * (pairs - 1) + 1 + (GROUP - 1) + (wide - 1))
+    pl.semaphore_wait(barrier, count - 1)
     for k in range(1, pairs):
         send_halo(k, behind_of[k]).start()
         send_init(k, ahead_of[k]).start()
@@ -562,26 +545,32 @@
         for n, part in enumerate(parts):
             row = jnp.where(lane == n, part, row)
 
-        def reduce_over(row, send_ref, recv_ref, s_sem, r_sem, me, peers, meanwhile):
-            count = len(peers)
-            send_ref[p] = row
-
-            def send(j, at, blk, rep):
-                return copy(
-                    send_ref.at[p], recv_ref.at[p, at], s_sem.at[p, j], r_sem.at[p, at], blk, rep
-                )
-
-            for j in range(1, count):
-                send(j, me, *peers[j]).start()
+        def reduce_all(row, meanwhile):
+            gsend[p] = row
+
+            def start(j, _):
+                pltpu.make_async_remote_copy(
+                    src_ref=gsend.at[p],
+                    dst_ref=grecv.at[p, me],
+                    send_sem=s_g.at[p],
+                    recv_sem=r_g.at[p],
+                    device_id=lax.rem(me + j, count),
+                    device_id_type=pl.DeviceIdType.LOGICAL,
+                ).start()
+                return 0
+
+            lax.fori_loop(1, count, start, 0, unroll=UJ)
             meanwhile()
-            later(1, count, lambda j: send(j, me, b, r).wait_send())
-            recv_ref[p, me] = row
-            for j in range(1, count):
-                send(j, lax.rem(me + j, count), b, r).wait_recv()
-            total = recv_ref[p, 0]
-            for n in range(1, count):
-                total = total + recv_ref[p, n]
-            return total
+            grecv[p, me] = row
+            rest = pltpu.make_async_copy(grecv.at[p, 1:count], grecv.at[p, 1:count], r_g.at[p])
+            rest.wait()
+            sent = pltpu.make_async_copy(grecv.at[p, 1:count], grecv.at[p, 1:count], s_g.at[p])
+            pending.append(sent.wait)
+            total = [grecv[p, n] for n in range(8)]
+            for n in range(8, count):
+                total[n % 8] = total[n % 8] + grecv[p, n]
+            total = [total[n] + total[n + 4] for n in range(4)]
+            return (total[0] + total[1]) + (total[2] + total[3])
 
         def write_weights():
             drain()
@@ -589,8 +578,7 @@
                 for t in range(tiles):
                     weights_out[0, k : k + 1, t * LANES : (t + 1) * LANES] = wout[k, t : t + 1]
 
-        row = reduce_over(row, g1send, g1recv, s_g1, r_g1, low, inner_of, drain)
-        row = reduce_over(row, g2send, g2recv, s_g2, r_g2, mine2, outer_of, write_weights)
+        row = reduce_all(row, write_weights)
 
         def scalar(n):
             return jnp.sum(jnp.where(lane == n, row, 0.0), axis=1, keepdims=True)
@@ -643,7 +631,6 @@
     cams = start_angles.shape[1]
     tiles = slots // LANES
     lo = cams // HI
-    wide = (n_blk // GROUP) * n_rep
     vmem = pltpu.VMEM
     sem = pltpu.SemaphoreType.DMA
 
@@ -685,9 +672,7 @@
         edges(2 * PASSES, 2, pairs, 3),
         edges(2 * PASSES, 2, pairs, 3),
         vmem((PASSES, 1, LANES), F32),
-        vmem((PASSES, GROUP, 1, LANES), F32),
-        vmem((PASSES, 1, LANES), F32),
-        vmem((PASSES, wide, 1, LANES), F32),
+        vmem((PASSES, n_blk * n_rep, 1, LANES), F32),
         vmem((2 * pairs, 18 * HI, slots), BF16),
         sem((3, pairs)),
         sem((3, pairs)),
@@ -697,10 +682,8 @@
         sem((PASSES,)),
         sem((2 * PASSES, 2, pairs)),
         sem((2 * PASSES, 2, pairs)),
-        sem((PASSES, GROUP)),
-        sem((PASSES, GROUP)),
-        sem((PASSES, wide)),
-        sem((PASSES, wide)),
+        sem((PASSES,)),
+        sem((PASSES,)),
         vmem(measured.shape, F32),
         vmem(rot_vector.shape, F32),
         vmem(confidence.shape, F32),

time: 84.4 us -> 82.6 us (0.979)
  Pallas kernels: 82.2 us -> 80.6 us
    pallas_call x1, Pallas kernels: 82.2 us -> 80.6 us  [on_device(): pl.pallas_call(functools.partial(kernel, n_blk, n_rep), out_shape=(pltpu....]
where the time goes in v4:
time: 82.6 us; the launch traced here: 82.4 us
  Pallas kernels  80.6 us (98%)
  local copies, waits for them, and re-layouts  1.22 us (1%)
    pallas_call x1, Pallas kernels, on_device(): pl.pallas_call(functools.partial(kernel, n_blk, n_rep), out_shape=(pltpu....  80.6 us

profile of v4, /device:TPU:1, one launch (start us, length us, event | category | flops | bytes accessed | tf_op | source)
XLA Modules:
  0.0 82.4 jit_solution(3756694313641302182)
XLA Ops:
  0.6 80.6 %shard_map.95 = (f32[3,2048]{1,0:T(4,128)S(1)}, f32[1,8,768]{2,1,0:T(8,128)S(1)}) custom-call(f32[3,1,8,768]{3,2,1,0:T(8,128)} %measured_in.1, f32[3,1,8,768]{3,2,1,0:T(8,128)} %rot_in.1, f32[3,1,8,768]{3,2,1,0:T(8,128)} %conf_in.1, s32[1,8,768]{2,1,0:T(8,128)} %first_in.1, s32[1,8,768]{2,1,0:T(8,128)} %second_in.1, s32[1,8]{1,0:T(1,128)} %bitcast.3, ...), custom_call_target="tpu_custom_call" | custom-call | tf_op jit(solution)/shard_map/pallas_call | solution.py:698
  81.2 0.6 copy.12
  81.8 0.6 copy.13

commit v5 on v4

--- a/solution.py
+++ b/solution.py
@@ -21,7 +21,7 @@
 UG = 8
 US = 4
 UB = 4
-UJ = 8
+UJ = 16
 
 
 def loop(first, last, body, init, unroll):
@@ -186,25 +186,21 @@
 
     lax.fori_loop(1, count, greet, 0, unroll=UJ)
 
-    for load in loads:
+    for load in loads[:4]:
         load.wait()
     slot = lax.broadcasted_iota(jnp.int32, (tiles, LANES), 0) * LANES
     slot = slot + lax.broadcasted_iota(jnp.int32, (tiles, LANES), 1)
+    for h in range(HI):
+        at = slice(h * lo_count, (h + 1) * lo_count)
+        for c in range(3):
+            est[c, h : h + 1] = start_ref[c : c + 1, at]
     for k in range(pairs):
         live[k] = jnp.where(slot < counts_ref[0:1, k : k + 1], 1.0, 0.0).astype(F32)
         for t in range(tiles):
             at = slice(t * LANES, (t + 1) * LANES)
-            idx[k, t : t + 1] = first_ref[0, k : k + 1, at]
             idx[2 * pairs + k, t : t + 1] = second_ref[0, k : k + 1, at]
             for c in range(3):
                 conf[k, c, t : t + 1] = conf_ref[c, 0, k : k + 1, at]
-                meas[k, c, t : t + 1] = measured_ref[c, 0, k : k + 1, at]
-                rotm[k, c, t : t + 1] = rot_ref[c, 0, k : k + 1, at]
-    for h in range(HI):
-        at = slice(h * lo_count, (h + 1) * lo_count)
-        anc[h : h + 1] = anchor_ref[0:1, at]
-        for c in range(3):
-            est[c, h : h + 1] = start_ref[c : c + 1, at]
 
     def stage1(k, _):
         for c in range(3):
@@ -229,6 +225,18 @@
     for k in range(1, pairs):
         send_halo(k, behind_of[k]).start()
         send_init(k, ahead_of[k]).start()
+
+    for load in loads[4:]:
+        load.wait()
+    for k in range(pairs):
+        for t in range(tiles):
+            at = slice(t * LANES, (t + 1) * LANES)
+            idx[k, t : t + 1] = first_ref[0, k : k + 1, at]
+            for c in range(3):
+                meas[k, c, t : t + 1] = measured_ref[c, 0, k : k + 1, at]
+                rotm[k, c, t : t + 1] = rot_ref[c, 0, k : k + 1, at]
+    for h in range(HI):
+        anc[h : h + 1] = anchor_ref[0:1, h * lo_count : (h + 1) * lo_count]
 
     def rotations(k, _):
         v = [rotm[k, c] for c in range(3)]
@@ -377,21 +385,20 @@
             )
 
     def exchange_start(x, table):
-        def step(i, _):
-            k = (i + 1) % pairs
-            turned = rotate(k, gather(table, k))
+        for k in range(1, pairs + 1):
+            k = k % pairs
             there = gather(table, pairs + k)
             for c in range(3):
-                xsend[x, 0, k, c] = turned[c]
                 xsend[x, 1, k, c] = there[c]
-
             if k != 0:
                 send_back(x, k, behind_of[k]).start()
+        for k in range(1, pairs + 1):
+            k = k % pairs
+            turned = rotate(k, gather(table, k))
+            for c in range(3):
+                xsend[x, 0, k, c] = turned[c]
+            if k != 0:
                 send_ahead(x, k, ahead_of[k]).start()
-
-            return 0
-
-        loop(0, pairs, step, 0, pairs)
         later(1, pairs, lambda k: (send_back(x, k, b).wait_send(), send_ahead(x, k, b).wait_send()))
         xrecv[x, 0, 0] = xsend[x, 0, 0]
         xrecv[x, 1, 0] = xsend[x, 1, 0]

time: 82.6 us -> 82.5 us (level)
  no operation moved by 1% of the time
where the time goes in v5:
time: 82.5 us; the launch traced here: 82.4 us
  Pallas kernels  80.5 us (98%)
  local copies, waits for them, and re-layouts  1.22 us (1%)
    pallas_call x1, Pallas kernels, on_device(): pl.pallas_call(functools.partial(kernel, n_blk, n_rep), out_shape=(pltpu....  80.5 us

profile of v5, /device:TPU:1, one launch (start us, length us, event | category | flops | bytes accessed | tf_op | source)
XLA Modules:
  0.0 82.4 jit_solution(16030177287299775145)
XLA Ops:
  0.6 80.5 %shard_map.95 = (f32[3,2048]{1,0:T(4,128)S(1)}, f32[1,8,768]{2,1,0:T(8,128)S(1)}) custom-call(f32[3,1,8,768]{3,2,1,0:T(8,128)} %measured_in.1, f32[3,1,8,768]{3,2,1,0:T(8,128)} %rot_in.1, f32[3,1,8,768]{3,2,1,0:T(8,128)} %conf_in.1, s32[1,8,768]{2,1,0:T(8,128)} %first_in.1, s32[1,8,768]{2,1,0:T(8,128)} %second_in.1, s32[1,8]{1,0:T(1,128)} %bitcast.3, ...), custom_call_target="tpu_custom_call" | custom-call | tf_op jit(solution)/shard_map/pallas_call | solution.py:705
  81.1 0.6 copy.12
  81.7 0.6 copy.13
